TPU v7x, 32 devices: a whole 2x2x4 slice. The times are simulated.
32 devices in a mesh: rep: 2 (over x), dp: 16 (over y, z, core).
Axes of the slice: x: 2, y: 2, z: 4, core: 2. Of those that a mesh axis runs over, the one named last changes fastest.
Arguments:
- x: bfloat16 [32, 2048, 1024], P(('rep', 'dp')), parts along dimension 0
- dy: bfloat16 [32, 2048, 1024], P(('rep', 'dp')), parts along dimension 0
- w_gate: bfloat16 [2, 1024, 3200], replicated
- w_up: bfloat16 [2, 1024, 3200], replicated
- w_down: bfloat16 [2, 3200, 1024], replicated
- m_w_gate: float32 [2, 1024, 3200], P(None, 'dp')
- m_w_up: float32 [2, 1024, 3200], P(None, 'dp')
- m_w_down: float32 [2, 3200, 1024], P(None, 'dp')
- v_w_gate: float32 [2, 1024, 3200], P(None, 'dp')
- v_w_up: float32 [2, 1024, 3200], P(None, 'dp')
- v_w_down: float32 [2, 3200, 1024], P(None, 'dp')
Outputs:
- output 1: bfloat16 [4, 1024, 3200], P('rep'), parts along dimension 0
- output 2: bfloat16 [4, 1024, 3200], P('rep'), parts along dimension 0
- output 3: bfloat16 [4, 3200, 1024], P('rep'), parts along dimension 0
- output 4: float32 [4, 1024, 3200], P('rep', 'dp'), parts along dimension 0
- output 5: float32 [4, 1024, 3200], P('rep', 'dp'), parts along dimension 0
- output 6: float32 [4, 3200, 1024], P('rep', 'dp'), parts along dimension 0
- output 7: float32 [4, 1024, 3200], P('rep', 'dp'), parts along dimension 0
- output 8: float32 [4, 1024, 3200], P('rep', 'dp'), parts along dimension 0
- output 9: float32 [4, 3200, 1024], P('rep', 'dp'), parts along dimension 0
There are 2 independent parts. A program takes and returns all parts, laid end to end along the dimension named above; an argument that names none is the same for every part.
All inputs are finite; a program needn't handle non-finite values.
Results may differ from a plain program's by a relative error of at most 0.022.
Values are sent between devices in bfloat16 or wider.
A program may use at most 2 GiB of HBM per device.

v0:
```python
import jax
import jax.numpy as jnp
from jax import lax

NAMES = ("w_gate", "w_up", "w_down")


def matmul(a, w):
    return jnp.dot(a, w, preferred_element_type=jnp.float32).astype(jnp.bfloat16)


def normed(h):
    wide = h.astype(jnp.float32)
    scale = lax.rsqrt(jnp.mean(wide**2, -1, keepdims=True) + 1e-6)
    return (wide * scale).astype(jnp.bfloat16)


def layer(h, w):
    a = normed(h)
    gate = jnp.dot(a, w["w_gate"], preferred_element_type=jnp.float32)
    up = jnp.dot(a, w["w_up"], preferred_element_type=jnp.float32)
    return h + matmul((jax.nn.silu(gate) * up).astype(jnp.bfloat16), w["w_down"])


def adamw(w, m, v, g):
    m = 0.9 * m + 0.1 * g
    v = 0.95 * v + 0.05 * g * g
    step = m * lax.rsqrt(v + 1e-8) + 0.1 * w
    return (w - 0.02 * step).astype(jnp.bfloat16), m, v


def stack(weights, h):
    for number in range(weights["w_gate"].shape[0]):
        h = layer(h, {name: w[number] for name, w in weights.items()})
    return h


def solution(mesh):
    groups = mesh.shape["rep"]

    def step(x, dy, *arrays):
        weights, m, v = (arrays[i : i + 3] for i in (0, 3, 6))
        x, dy = (t.reshape(groups, -1, *t.shape[1:]) for t in (x, dy))

        def of_a_group(x, dy):
            _, back = jax.vjp(lambda w: stack(w, x), dict(zip(NAMES, weights, strict=True)))
            by_weights = back(dy)[0]
            gradients = [by_weights[name].astype(jnp.float32) for name in NAMES]
            new = [adamw(w.astype(jnp.float32), m, v, g) for w, m, v, g in zip(weights, m, v, gradients, strict=True)]
            return tuple(one[which] for which in range(3) for one in new)

        return tuple(t.reshape(-1, *t.shape[2:]) for t in jax.vmap(of_a_group)(x, dy))

    return step
```

profile of v0, /device:TPU:0, one launch (start us, length us, event | category | flops | bytes accessed | tf_op | source)
XLA Modules:
  0.0 1757.0 jit_solution(15919328397117693650)
XLA Ops:
  22.5 20.9 %fusion.188 = f32[2048,3200]{1,0:T(8,128)} fusion(bf16[2,1024,3200]{2,1,0:T(8,128)(2,1)} %param.12, bf16[1,2048,1024]{2,1,0:T(8,128)(2,1)S(1)} %copy-done.11, f32[2048]{0:T(1024)S(1)} %add_rsqrt_fusion), kind=kOutput, calls=%fused_computation.228 | convolution fusion | flops 13428064256 | bytes 36970496 | tf_op jit(solution)/vmap(jvp())/dot_general | solution.py:20
  43.5 32.1 %fusion.164 = (bf16[1,1,2048,3200]{3,2,1,0:T(8,128)(2,1)}, f32[2048,3200]{1,0:T(8,128)}) fusion(f32[2048,3200]{1,0:T(8,128)} %fusion.188, bf16[2,1024,3200]{2,1,0:T(8,128)(2,1)} %param.15, bf16[1,2048,1024]{2,1,0:T(8,128)(2,1)} %param.14, f32[2048]{0:T(1024)S(1)} %add_rsqrt_fusion), kind=kOutput, calls=%fused_computation.191 | convolution fusion | flops 13467385856 | bytes 76292096 | tf_op jit(solution)/vmap(jvp())/dot_general | solution.py:21
  75.5 22.3 %fusion.174 = (f32[2048]{0:T(1024)S(1)}, bf16[1,1,2048,1024]{2,3,1,0:T(8,128)(2,1)}) fusion(bf16[2,3200,1024]{2,1,0:T(8,128)(2,1)} %param.16, bf16[1,1,2048,3200]{3,2,1,0:T(8,128)(2,1)} %get-tuple-element.263, bf16[1,2048,1024]{1,2,0:T(8,128)(2,1)} %copy), kind=kOutput, calls=%fused_computation.213 | convolution fusion | flops 13432256512 | bytes 28057600 | tf_op jit(solution)/vmap(jvp())/dot_general | solution.py:9
  101.8 22.3 %fusion.177 = f32[2048,3200]{1,0:T(8,128)} fusion(bf16[2,1024,3200]{2,1,0:T(8,128)(2,1)} %param.12, bf16[1,1,2048,1024]{2,3,1,0:T(8,128)(2,1)S(1)} %fusion.175), kind=kOutput, calls=%fused_computation.217 | convolution fusion | flops 13421772800 | bytes 36962304 | tf_op jit(solution)/vmap(jvp())/dot_general | solution.py:20
  124.1 30.0 %fusion.163 = (bf16[1,1,2048,3200]{3,2,1,0:T(8,128)(2,1)}, f32[2048,3200]{1,0:T(8,128)}) fusion(f32[2048,3200]{1,0:T(8,128)} %fusion.177, bf16[2,1024,3200]{2,1,0:T(8,128)(2,1)} %param.15, bf16[1,1,2048,1024]{2,3,1,0:T(8,128)(2,1)S(1)} %fusion.175), kind=kOutput, calls=%fused_computation.189 | convolution fusion | flops 13461094400 | bytes 76283904 | tf_op jit(solution)/vmap(jvp())/dot_general | solution.py:21
  160.7 39.0 %convert_multiply_fusion.2 = (bf16[1,1,2048,3200]{3,2,1,0:T(8,128)(2,1)}, bf16[1,1,2048,3200]{3,2,1,0:T(8,128)(2,1)}) fusion(f32[2048,3200]{1,0:T(8,128)} %fusion.177, f32[2048,3200]{1,0:T(8,128)} %get-tuple-element.270, bf16[2,3200,1024]{2,1,0:T(8,128)(2,1)} %param.16, bf16[1,2048,1024]{2,1,0:T(8,128)(2,1)} %param.17), kind=kOutput, calls=%fused_computation.172 | convolution fusion | flops 13526630400 | bytes 89391104 | tf_op jit(solution)/vmap(transpose(jvp()))/dot_general | solution.py:9
  199.7 19.9 %fusion.156 = bf16[2048,1024]{0,1:T(8,128)(2,1)} fusion(bf16[1,1,2048,3200]{3,2,1,0:T(8,128)(2,1)} %get-tuple-element.545, bf16[2,1024,3200]{2,1,0:T(8,128)(2,1)} %param.12), kind=kOutput, calls=%fused_computation.178 | convolution fusion | flops 13421772800 | bytes 23855104 | tf_op jit(solution)/vmap(transpose(jvp()))/dot_general | solution.py:20
  219.6 21.6 %fusion.176 = (f32[2048]{0:T(1024)S(1)}, bf16[2048,1024]{0,1:T(8,128)(2,1)}) fusion(bf16[1,1,2048,1024]{2,3,1,0:T(8,128)(2,1)S(1)} %copy-done.9, bf16[2048,1024]{0,1:T(8,128)(2,1)} %fusion.156, bf16[2,1024,3200]{2,1,0:T(8,128)(2,1)} %param.15, bf16[1,1,2048,3200]{3,2,1,0:T(8,128)(2,1)} %get-tuple-element.623), kind=kOutput, calls=%fused_computation.215 | convolution fusion | flops 13432256512 | bytes 32251904 | tf_op jit(solution)/vmap(transpose(jvp()))/dot_general | solution.py:21
  247.9 36.6 %convert_multiply_fusion = (bf16[1,1,2048,3200]{3,2,1,0:T(8,128)(2,1)}, bf16[1,1,2048,3200]{3,2,1,0:T(8,128)(2,1)}) fusion(f32[2048,3200]{1,0:T(8,128)} %fusion.188, f32[2048,3200]{1,0:T(8,128)} %get-tuple-element.264, bf16[2,3200,1024]{2,1,0:T(8,128)(2,1)} %param.16, bf16[1,1,2048,1024]{2,3,1,0:T(8,128)(2,1)S(1)} %fusion.199), kind=kOutput, calls=%fused_computation.170 | convolution fusion | flops 13526630400 | bytes 89391104 | tf_op jit(solution)/vmap(transpose(jvp()))/dot_general | solution.py:9
  284.5 164.2 %while.13 = (bf16[1,1,2048,1024]{2,3,1,0:T(8,128)(2,1)}, bf16[1,1,2048,3200]{3,2,1,0:T(8,128)(2,1)}, f32[1,64,3200]{2,1,0:T(8,128)S(1)}, f32[1,64,3200]{2,1,0:T(...) while((bf16[1,1,2048,1024]{2,3,1,0:T(8,128)(2,1)}, ...), condition=%wide.windowed_dot_general_cond_rs.1.clone, body=%wide.windowed_dot_general_body_rs.1.clone.sunk | while | flops 3358769152 | bytes 120193760 | solution.py:20
  313.0 14.1 collective-permute-done.6
  356.4 13.2 collective-permute-done.6
  453.2 195.5 %while.12 = (bf16[1,1,2048,1024]{2,3,1,0:T(8,128)(2,1)}, bf16[1,1,2048,3200]{3,2,1,0:T(8,128)(2,1)}, f32[1,64,3200]{2,1,0:T(8,128)S(1)}, f32[1,64,3200]{2,1,0:T(...) while((bf16[1,1,2048,1024]{2,3,1,0:T(8,128)(2,1)}, ...), condition=%wide.windowed_dot_general_cond_rs.clone, body=%wide.windowed_dot_general_body_rs.clone.sunk | while | flops 3358769152 | bytes 120193760 | solution.py:20
  536.1 16.0 collective-permute-done.2
  584.5 13.4 collective-permute-done.2
  631.2 16.4 collective-permute-done.2
  648.8 196.7 %while.15 = (bf16[1,1,2048,1024]{2,3,1,0:T(8,128)(2,1)}, bf16[1,1,2048,3200]{3,2,1,0:T(8,128)(2,1)}, f32[1,64,3200]{2,1,0:T(8,128)S(1)}, f32[1,64,3200]{2,1,0:T(...) while((bf16[1,1,2048,1024]{2,3,1,0:T(8,128)(2,1)}, ...), condition=%wide.windowed_dot_general_cond_rs.3.clone, body=%wide.windowed_dot_general_body_rs.3.clone.sunk | while | flops 3358769152 | bytes 120193760 | solution.py:21
  664.9 15.8 collective-permute-done.12
  687.5 12.3 collective-permute-done.14
  731.5 16.0 collective-permute-done.14
  780.0 13.4 collective-permute-done.14
  827.6 16.8 collective-permute-done.14
  853.7 260.3 %while.14 = (bf16[1,1,2048,1024]{2,3,1,0:T(8,128)(2,1)}, bf16[1,1,2048,3200]{3,2,1,0:T(8,128)(2,1)}, f32[1,64,3200]{2,1,0:T(8,128)S(1)}, f32[1,64,3200]{2,1,0:T(...) while((bf16[1,1,2048,1024]{2,3,1,0:T(8,128)(2,1)}, ...), condition=%wide.windowed_dot_general_cond_rs.2.clone, body=%wide.windowed_dot_general_body_rs.2.clone.sunk | while | flops 3358769152 | bytes 120193760 | solution.py:21
  876.4 34.5 %collective-permute-start.10 = (f32[1,64,3200]{2,1,0:T(8,128)S(1)}, f32[1,64,3200]{2,1,0:T(8,128)S(1)}, u32[]{:S(2)}, u32[]{:S(2)}) collective-permute-start(f32[1,64,3200]{2,1,0:T(8,128)S(1)} %get-tuple-element.474), channel_id=18, source_target_pairs={{0,1},{1,2},{2,3},{3,4},{4,5},{5,6},{6,7},{7,8},{8,9},{9,10},{10,1... | collective-permute-start | bytes 2457608 | tf_op jit(solution)/vmap(transpose(jvp()))/dot_general | solution.py:21
  916.9 12.3 collective-permute-done.11
  944.7 25.3 %collective-permute-done.8 = f32[1,64,3200]{2,1,0:T(8,128)S(1)} collective-permute-done((f32[1,64,3200]{2,1,0:T(8,128)S(1)}, f32[1,64,3200]{2,1,0:T(8,128)S(1)}, u32[]{:S(2)}, u32[]{:S(2)}) %collective-permute-start.8) | collective-permute-done | bytes 819232 | tf_op jit(solution)/vmap(transpose(jvp()))/dot_general | solution.py:21
  970.2 35.4 %collective-permute-start.10 = (f32[1,64,3200]{2,1,0:T(8,128)S(1)}, f32[1,64,3200]{2,1,0:T(8,128)S(1)}, u32[]{:S(2)}, u32[]{:S(2)}) collective-permute-start(f32[1,64,3200]{2,1,0:T(8,128)S(1)} %get-tuple-element.474), channel_id=18, source_target_pairs={{0,1},{1,2},{2,3},{3,4},{4,5},{5,6},{6,7},{7,8},{8,9},{9,10},{10,1... | collective-permute-start | bytes 2457608 | tf_op jit(solution)/vmap(transpose(jvp()))/dot_general | solution.py:21
  1010.8 12.8 collective-permute-done.11
  1052.8 15.7 collective-permute-done.10
  1097.6 16.2 collective-permute-done.10
  1115.5 13.1 collective-permute-done.26
  1132.7 18.2 %copy.4 = bf16[1,1,2048,3200]{2,3,1,0:T(8,128)(2,1)} copy(bf16[1,1,2048,3200]{3,2,1,0:T(8,128)(2,1)} %get-tuple-element.263) | data formatting | bytes 26214400
  1157.3 233.1 %while.17 = (bf16[1,1,2048,3200]{2,3,1,0:T(8,128)(2,1)}, bf16[1,1,2048,1024]{3,2,1,0:T(8,128)(2,1)}, f32[1,200,1024]{2,1,0:T(8,128)S(1)}, f32[1,200,1024]{2,1,0:...) while((bf16[1,1,2048,3200]{2,3,1,0:T(8,128)(2,1)}, ...), condition=%wide.windowed_dot_general_cond_rs.5.clone, body=%wide.windowed_dot_general_body_rs.5.clone.sunk | while | flops 3363225600 | bytes 64094820 | solution.py:9
  1169.5 17.1 collective-permute-done.20
  1196.6 25.1 %collective-permute-done.22 = f32[1,200,1024]{2,1,0:T(8,128)S(1)} collective-permute-done((f32[1,200,1024]{2,1,0:T(8,128)S(1)}, f32[1,200,1024]{2,1,0:T(8,128)S(1)}, u32[]{:S(2)}, u32[]{:S(2)}) %collective-permute-start.22) | collective-permute-done | bytes 819232 | tf_op jit(solution)/vmap(transpose(jvp()))/dot_general | solution.py:9
  1224.1 10.4 collective-permute-start.20
  1242.1 22.8 %collective-permute-done.20 = f32[1,200,1024]{2,1,0:T(8,128)S(1)} collective-permute-done((f32[1,200,1024]{2,1,0:T(8,128)S(1)}, f32[1,200,1024]{2,1,0:T(8,128)S(1)}, u32[]{:S(2)}, u32[]{:S(2)}) %collective-permute-start.20) | collective-permute-done | bytes 819232 | tf_op jit(solution)/vmap(transpose(jvp()))/dot_general | solution.py:9
  1270.1 10.4 collective-permute-start.22
  1332.7 12.8 collective-permute-done.22
  1390.5 18.5 %copy.2 = bf16[1,1,2048,3200]{2,3,1,0:T(8,128)(2,1)} copy(bf16[1,1,2048,3200]{3,2,1,0:T(8,128)(2,1)} %get-tuple-element.269) | data formatting | bytes 26214400
  1415.4 186.5 %while.16 = (bf16[1,1,2048,3200]{2,3,1,0:T(8,128)(2,1)}, bf16[1,1,2048,1024]{3,2,1,0:T(8,128)(2,1)}, f32[1,200,1024]{2,1,0:T(8,128)S(1)}, f32[1,200,1024]{2,1,0:...) while((bf16[1,1,2048,3200]{2,3,1,0:T(8,128)(2,1)}, ...), condition=%wide.windowed_dot_general_cond_rs.4.clone, body=%wide.windowed_dot_general_body_rs.4.clone.sunk | while | flops 3363225600 | bytes 64094820 | solution.py:9
  1448.2 12.9 collective-permute-done.18
  1476.5 10.0 collective-permute-done.16
  1497.6 10.0 collective-permute-done.18
  1543.9 10.0 collective-permute-done.18
  1603.3 13.0 collective-permute-done.28
  1620.6 102.6 %all-gather.14.cloned.1.call-done = bf16[1,2,3200,1024]{3,2,1,0:T(8,128)(2,1)} async-done(((bf16[1,2,200,1024]{3,2,1,0:T(8,128)(2,1)}), bf16[1,2,3200,1024]{3,2,1,0:T(8,128)(2,1)}) %all-gather.14.cloned.1.call-update) | async-done | bytes 13107216 | tf_op jit(solution)/reshape | solution.py:52
  1723.2 12.7 copy.63
  (612 shorter events, 827.6 us)
Async XLA Ops:
  7.2 1613.4 %all-gather.10.cloned.1.call-start = ((), (), s32[]{:S(2)}) async-start(), calls=%async_computation | async-start | bytes 13926400 | tf_op jit(solution)/reshape | solution.py:52
  448.7 398.3 %collective-permute-start.25 = (f32[1,64,3200]{2,1,0:T(8,128)}, f32[1,64,3200]{2,1,0:T(8,128)}, u32[]{:S(2)}, u32[]{:S(2)}) collective-permute-start(f32[1,64,3200]{2,1,0:T(8,128)} %get-tuple-element.39), channel_id=12, source_target_pairs={{0,1},{1,2},{2,3},{3,4},{4,5},{5,6},{6,7},{7,8},{8,9},{9,10},{10,1... | collective-permute-start | bytes 2457608 | tf_op jit(solution)/vmap(transpose(jvp()))/dot_general | solution.py:20
  454.3 22.3 %collective-permute-start = (f32[1,64,3200]{2,1,0:T(8,128)}, f32[1,64,3200]{2,1,0:T(8,128)S(1)}, u32[]{:S(2)}, u32[]{:S(2)}) collective-permute-start(f32[1,64,3200]{2,1,0:T(8,128)} %broadcast_select_fusion.24), channel_id=3, source_target_pairs={{0,1},{1,2},{2,3},{3,4},{4,5},{5,6},{6,7},{7,8},{8,9},{9,10},{10,1... | collective-permute-start | bytes 2457608 | tf_op jit(solution)/vmap(transpose(jvp()))/dot_general | solution.py:20
  456.1 22.2 %collective-permute-start.1 = (f32[1,64,3200]{2,1,0:T(8,128)}, f32[1,64,3200]{2,1,0:T(8,128)S(1)}, u32[]{:S(2)}, u32[]{:S(2)}) collective-permute-start(f32[1,64,3200]{2,1,0:T(8,128)} %broadcast_select_fusion.25), channel_id=2, source_target_pairs={{0,15},{1,0},{2,1},{3,2},{4,3},{5,4},{6,5},{7,6},{8,7},{9,8},{10,9... | collective-permute-start | bytes 2457608 | tf_op jit(solution)/vmap(transpose(jvp()))/dot_general | solution.py:20
  503.9 21.8 %collective-permute-start = (f32[1,64,3200]{2,1,0:T(8,128)}, f32[1,64,3200]{2,1,0:T(8,128)S(1)}, u32[]{:S(2)}, u32[]{:S(2)}) collective-permute-start(f32[1,64,3200]{2,1,0:T(8,128)} %broadcast_select_fusion.24), channel_id=3, source_target_pairs={{0,1},{1,2},{2,3},{3,4},{4,5},{5,6},{6,7},{7,8},{8,9},{9,10},{10,1... | collective-permute-start | bytes 2457608 | tf_op jit(solution)/vmap(transpose(jvp()))/dot_general | solution.py:20
  529.4 22.8 %collective-permute-start.2 = (f32[1,64,3200]{2,1,0:T(8,128)S(1)}, f32[1,64,3200]{2,1,0:T(8,128)S(1)}, u32[]{:S(2)}, u32[]{:S(2)}) collective-permute-start(f32[1,64,3200]{2,1,0:T(8,128)S(1)} %get-tuple-element.456), channel_id=5, source_target_pairs={{0,1},{1,2},{2,3},{3,4},{4,5},{5,6},{6,7},{7,8},{8,9},{9,10},{10,1... | collective-permute-start | bytes 2457608 | tf_op jit(solution)/vmap(transpose(jvp()))/dot_general | solution.py:20
  529.4 22.7 %collective-permute-start.3 = (f32[1,64,3200]{2,1,0:T(8,128)S(1)}, f32[1,64,3200]{2,1,0:T(8,128)S(1)}, u32[]{:S(2)}, u32[]{:S(2)}) collective-permute-start(f32[1,64,3200]{2,1,0:T(8,128)S(1)} %get-tuple-element.457), channel_id=4, source_target_pairs={{0,15},{1,0},{2,1},{3,2},{4,3},{5,4},{6,5},{7,6},{8,7},{9,8},{10,9... | collective-permute-start | bytes 2457608 | tf_op jit(solution)/vmap(transpose(jvp()))/dot_general | solution.py:20
  555.3 22.5 %collective-permute-start = (f32[1,64,3200]{2,1,0:T(8,128)}, f32[1,64,3200]{2,1,0:T(8,128)S(1)}, u32[]{:S(2)}, u32[]{:S(2)}) collective-permute-start(f32[1,64,3200]{2,1,0:T(8,128)} %broadcast_select_fusion.24), channel_id=3, source_target_pairs={{0,1},{1,2},{2,3},{3,4},{4,5},{5,6},{6,7},{7,8},{8,9},{9,10},{10,1... | collective-permute-start | bytes 2457608 | tf_op jit(solution)/vmap(transpose(jvp()))/dot_general | solution.py:20
  602.7 21.8 %collective-permute-start = (f32[1,64,3200]{2,1,0:T(8,128)}, f32[1,64,3200]{2,1,0:T(8,128)S(1)}, u32[]{:S(2)}, u32[]{:S(2)}) collective-permute-start(f32[1,64,3200]{2,1,0:T(8,128)} %broadcast_select_fusion.24), channel_id=3, source_target_pairs={{0,1},{1,2},{2,3},{3,4},{4,5},{5,6},{6,7},{7,8},{8,9},{9,10},{10,1... | collective-permute-start | bytes 2457608 | tf_op jit(solution)/vmap(transpose(jvp()))/dot_general | solution.py:20
  624.7 22.9 %collective-permute-start.2 = (f32[1,64,3200]{2,1,0:T(8,128)S(1)}, f32[1,64,3200]{2,1,0:T(8,128)S(1)}, u32[]{:S(2)}, u32[]{:S(2)}) collective-permute-start(f32[1,64,3200]{2,1,0:T(8,128)S(1)} %get-tuple-element.456), channel_id=5, source_target_pairs={{0,1},{1,2},{2,3},{3,4},{4,5},{5,6},{6,7},{7,8},{8,9},{9,10},{10,1... | collective-permute-start | bytes 2457608 | tf_op jit(solution)/vmap(transpose(jvp()))/dot_general | solution.py:20
  624.8 22.9 %collective-permute-start.3 = (f32[1,64,3200]{2,1,0:T(8,128)S(1)}, f32[1,64,3200]{2,1,0:T(8,128)S(1)}, u32[]{:S(2)}, u32[]{:S(2)}) collective-permute-start(f32[1,64,3200]{2,1,0:T(8,128)S(1)} %get-tuple-element.457), channel_id=4, source_target_pairs={{0,15},{1,0},{2,1},{3,2},{4,3},{5,4},{6,5},{7,6},{8,7},{9,8},{10,9... | collective-permute-start | bytes 2457608 | tf_op jit(solution)/vmap(transpose(jvp()))/dot_general | solution.py:20
  648.7 199.6 %collective-permute-start.24 = (f32[1,64,3200]{2,1,0:T(8,128)}, f32[1,64,3200]{2,1,0:T(8,128)}, u32[]{:S(2)}, u32[]{:S(2)}) collective-permute-start(f32[1,64,3200]{2,1,0:T(8,128)} %get-tuple-element.37), channel_id=6, source_target_pairs={{0,1},{1,2},{2,3},{3,4},{4,5},{5,6},{6,7},{7,8},{8,9},{9,10},{10,1... | collective-permute-start | bytes 2457608 | tf_op jit(solution)/vmap(transpose(jvp()))/dot_general | solution.py:20
  649.7 31.0 %collective-permute-start.12 = (f32[1,64,3200]{2,1,0:T(8,128)}, f32[1,64,3200]{2,1,0:T(8,128)S(1)}, u32[]{:S(2)}, u32[]{:S(2)}) collective-permute-start(f32[1,64,3200]{2,1,0:T(8,128)} %broadcast_select_fusion.30), channel_id=22, source_target_pairs={{0,1},{1,2},{2,3},{3,4},{4,5},{5,6},{6,7},{7,8},{8,9},{9,10},{10,1... | collective-permute-start | bytes 2457608 | tf_op jit(solution)/vmap(transpose(jvp()))/dot_general | solution.py:21
  650.7 30.0 %collective-permute-start.13 = (f32[1,64,3200]{2,1,0:T(8,128)}, f32[1,64,3200]{2,1,0:T(8,128)S(1)}, u32[]{:S(2)}, u32[]{:S(2)}) collective-permute-start(f32[1,64,3200]{2,1,0:T(8,128)} %broadcast_select_fusion.31), channel_id=21, source_target_pairs={{0,15},{1,0},{2,1},{3,2},{4,3},{5,4},{6,5},{7,6},{8,7},{9,8},{10,9... | collective-permute-start | bytes 2457608 | tf_op jit(solution)/vmap(transpose(jvp()))/dot_general | solution.py:21
  724.9 22.7 %collective-permute-start.14 = (f32[1,64,3200]{2,1,0:T(8,128)S(1)}, f32[1,64,3200]{2,1,0:T(8,128)S(1)}, u32[]{:S(2)}, u32[]{:S(2)}) collective-permute-start(f32[1,64,3200]{2,1,0:T(8,128)S(1)} %get-tuple-element.483), channel_id=24, source_target_pairs={{0,1},{1,2},{2,3},{3,4},{4,5},{5,6},{6,7},{7,8},{8,9},{9,10},{10,1... | collective-permute-start | bytes 2457608 | tf_op jit(solution)/vmap(transpose(jvp()))/dot_general | solution.py:21
  724.9 22.6 %collective-permute-start.15 = (f32[1,64,3200]{2,1,0:T(8,128)S(1)}, f32[1,64,3200]{2,1,0:T(8,128)S(1)}, u32[]{:S(2)}, u32[]{:S(2)}) collective-permute-start(f32[1,64,3200]{2,1,0:T(8,128)S(1)} %get-tuple-element.484), channel_id=23, source_target_pairs={{0,15},{1,0},{2,1},{3,2},{4,3},{5,4},{6,5},{7,6},{8,7},{9,8},{10,9... | collective-permute-start | bytes 2457608 | tf_op jit(solution)/vmap(transpose(jvp()))/dot_general | solution.py:21
  750.7 22.5 %collective-permute-start.12 = (f32[1,64,3200]{2,1,0:T(8,128)}, f32[1,64,3200]{2,1,0:T(8,128)S(1)}, u32[]{:S(2)}, u32[]{:S(2)}) collective-permute-start(f32[1,64,3200]{2,1,0:T(8,128)} %broadcast_select_fusion.30), channel_id=22, source_target_pairs={{0,1},{1,2},{2,3},{3,4},{4,5},{5,6},{6,7},{7,8},{8,9},{9,10},{10,1... | collective-permute-start | bytes 2457608 | tf_op jit(solution)/vmap(transpose(jvp()))/dot_general | solution.py:21
  799.0 21.8 %collective-permute-start.12 = (f32[1,64,3200]{2,1,0:T(8,128)}, f32[1,64,3200]{2,1,0:T(8,128)S(1)}, u32[]{:S(2)}, u32[]{:S(2)}) collective-permute-start(f32[1,64,3200]{2,1,0:T(8,128)} %broadcast_select_fusion.30), channel_id=22, source_target_pairs={{0,1},{1,2},{2,3},{3,4},{4,5},{5,6},{6,7},{7,8},{8,9},{9,10},{10,1... | collective-permute-start | bytes 2457608 | tf_op jit(solution)/vmap(transpose(jvp()))/dot_general | solution.py:21
  821.1 23.3 %collective-permute-start.14 = (f32[1,64,3200]{2,1,0:T(8,128)S(1)}, f32[1,64,3200]{2,1,0:T(8,128)S(1)}, u32[]{:S(2)}, u32[]{:S(2)}) collective-permute-start(f32[1,64,3200]{2,1,0:T(8,128)S(1)} %get-tuple-element.483), channel_id=24, source_target_pairs={{0,1},{1,2},{2,3},{3,4},{4,5},{5,6},{6,7},{7,8},{8,9},{9,10},{10,1... | collective-permute-start | bytes 2457608 | tf_op jit(solution)/vmap(transpose(jvp()))/dot_general | solution.py:21
  821.2 23.2 %collective-permute-start.15 = (f32[1,64,3200]{2,1,0:T(8,128)S(1)}, f32[1,64,3200]{2,1,0:T(8,128)S(1)}, u32[]{:S(2)}, u32[]{:S(2)}) collective-permute-start(f32[1,64,3200]{2,1,0:T(8,128)S(1)} %get-tuple-element.484), channel_id=23, source_target_pairs={{0,15},{1,0},{2,1},{3,2},{4,3},{5,4},{6,5},{7,6},{8,7},{9,8},{10,9... | collective-permute-start | bytes 2457608 | tf_op jit(solution)/vmap(transpose(jvp()))/dot_general | solution.py:21
  845.5 268.6 %collective-permute-start.27 = (f32[1,64,3200]{2,1,0:T(8,128)}, f32[1,64,3200]{2,1,0:T(8,128)}, u32[]{:S(2)}, u32[]{:S(2)}) collective-permute-start(f32[1,64,3200]{2,1,0:T(8,128)} %get-tuple-element.43), channel_id=25, source_target_pairs={{0,1},{1,2},{2,3},{3,4},{4,5},{5,6},{6,7},{7,8},{8,9},{9,10},{10,1... | collective-permute-start | bytes 2457608 | tf_op jit(solution)/vmap(transpose(jvp()))/dot_general | solution.py:21
  853.6 766.9 %all-gather.12.cloned.1.call-start = ((), (), s32[]{:S(2)}) async-start(), calls=%async_computation.1 | async-start | bytes 13926400 | tf_op jit(solution)/reshape | solution.py:52
  854.0 22.1 %collective-permute-start.8 = (f32[1,64,3200]{2,1,0:T(8,128)S(1)}, f32[1,64,3200]{2,1,0:T(8,128)S(1)}, u32[]{:S(2)}, u32[]{:S(2)}) collective-permute-start(f32[1,64,3200]{2,1,0:T(8,128)S(1)} %broadcast_select_fusion.28), channel_id=16, source_target_pairs={{0,1},{1,2},{2,3},{3,4},{4,5},{5,6},{6,7},{7,8},{8,9},{9,10},{10,1... | collective-permute-start | bytes 2457608 | tf_op jit(solution)/vmap(transpose(jvp()))/dot_general | solution.py:21
  876.4 40.5 %collective-permute-start.10 = (f32[1,64,3200]{2,1,0:T(8,128)S(1)}, f32[1,64,3200]{2,1,0:T(8,128)S(1)}, u32[]{:S(2)}, u32[]{:S(2)}) collective-permute-start(f32[1,64,3200]{2,1,0:T(8,128)S(1)} %get-tuple-element.474), channel_id=18, source_target_pairs={{0,1},{1,2},{2,3},{3,4},{4,5},{5,6},{6,7},{7,8},{8,9},{9,10},{10,1... | collective-permute-start | bytes 2457608 | tf_op jit(solution)/vmap(transpose(jvp()))/dot_general | solution.py:21
  929.5 40.5 %collective-permute-start.8 = (f32[1,64,3200]{2,1,0:T(8,128)S(1)}, f32[1,64,3200]{2,1,0:T(8,128)S(1)}, u32[]{:S(2)}, u32[]{:S(2)}) collective-permute-start(f32[1,64,3200]{2,1,0:T(8,128)S(1)} %broadcast_select_fusion.28), channel_id=16, source_target_pairs={{0,1},{1,2},{2,3},{3,4},{4,5},{5,6},{6,7},{7,8},{8,9},{9,10},{10,1... | collective-permute-start | bytes 2457608 | tf_op jit(solution)/vmap(transpose(jvp()))/dot_general | solution.py:21
  932.7 37.3 %collective-permute-start.9 = (f32[1,64,3200]{2,1,0:T(8,128)}, f32[1,64,3200]{2,1,0:T(8,128)S(1)}, u32[]{:S(2)}, u32[]{:S(2)}) collective-permute-start(f32[1,64,3200]{2,1,0:T(8,128)} %broadcast_select_fusion.29), channel_id=15, source_target_pairs={{0,15},{1,0},{2,1},{3,2},{4,3},{5,4},{6,5},{7,6},{8,7},{9,8},{10,9... | collective-permute-start | bytes 2457608 | tf_op jit(solution)/vmap(transpose(jvp()))/dot_general | solution.py:21
  970.2 40.6 %collective-permute-start.10 = (f32[1,64,3200]{2,1,0:T(8,128)S(1)}, f32[1,64,3200]{2,1,0:T(8,128)S(1)}, u32[]{:S(2)}, u32[]{:S(2)}) collective-permute-start(f32[1,64,3200]{2,1,0:T(8,128)S(1)} %get-tuple-element.474), channel_id=18, source_target_pairs={{0,1},{1,2},{2,3},{3,4},{4,5},{5,6},{6,7},{7,8},{8,9},{9,10},{10,1... | collective-permute-start | bytes 2457608 | tf_op jit(solution)/vmap(transpose(jvp()))/dot_general | solution.py:21
  1023.8 21.9 %collective-permute-start.8 = (f32[1,64,3200]{2,1,0:T(8,128)S(1)}, f32[1,64,3200]{2,1,0:T(8,128)S(1)}, u32[]{:S(2)}, u32[]{:S(2)}) collective-permute-start(f32[1,64,3200]{2,1,0:T(8,128)S(1)} %broadcast_select_fusion.28), channel_id=16, source_target_pairs={{0,1},{1,2},{2,3},{3,4},{4,5},{5,6},{6,7},{7,8},{8,9},{9,10},{10,1... | collective-permute-start | bytes 2457608 | tf_op jit(solution)/vmap(transpose(jvp()))/dot_general | solution.py:21
  1045.9 22.6 %collective-permute-start.10 = (f32[1,64,3200]{2,1,0:T(8,128)S(1)}, f32[1,64,3200]{2,1,0:T(8,128)S(1)}, u32[]{:S(2)}, u32[]{:S(2)}) collective-permute-start(f32[1,64,3200]{2,1,0:T(8,128)S(1)} %get-tuple-element.474), channel_id=18, source_target_pairs={{0,1},{1,2},{2,3},{3,4},{4,5},{5,6},{6,7},{7,8},{8,9},{9,10},{10,1... | collective-permute-start | bytes 2457608 | tf_op jit(solution)/vmap(transpose(jvp()))/dot_general | solution.py:21
  1069.0 21.9 %collective-permute-start.8 = (f32[1,64,3200]{2,1,0:T(8,128)S(1)}, f32[1,64,3200]{2,1,0:T(8,128)S(1)}, u32[]{:S(2)}, u32[]{:S(2)}) collective-permute-start(f32[1,64,3200]{2,1,0:T(8,128)S(1)} %broadcast_select_fusion.28), channel_id=16, source_target_pairs={{0,1},{1,2},{2,3},{3,4},{4,5},{5,6},{6,7},{7,8},{8,9},{9,10},{10,1... | collective-permute-start | bytes 2457608 | tf_op jit(solution)/vmap(transpose(jvp()))/dot_general | solution.py:21
  1091.1 22.7 %collective-permute-start.10 = (f32[1,64,3200]{2,1,0:T(8,128)S(1)}, f32[1,64,3200]{2,1,0:T(8,128)S(1)}, u32[]{:S(2)}, u32[]{:S(2)}) collective-permute-start(f32[1,64,3200]{2,1,0:T(8,128)S(1)} %get-tuple-element.474), channel_id=18, source_target_pairs={{0,1},{1,2},{2,3},{3,4},{4,5},{5,6},{6,7},{7,8},{8,9},{9,10},{10,1... | collective-permute-start | bytes 2457608 | tf_op jit(solution)/vmap(transpose(jvp()))/dot_general | solution.py:21
  1132.7 590.6 %all-gather.14.cloned.1.call-start = ((), (), s32[]{:S(2)}) async-start(), calls=%async_computation.2 | async-start | bytes 13926400 | tf_op jit(solution)/reshape | solution.py:52
  1157.4 29.1 %collective-permute-start.20 = (f32[1,200,1024]{2,1,0:T(8,128)S(1)}, f32[1,200,1024]{2,1,0:T(8,128)S(1)}, u32[]{:S(2)}, u32[]{:S(2)}) collective-permute-start(f32[1,200,1024]{2,1,0:T(8,128)S(1)} %broadcast_select_fusion.34), channel_id=35, source_target_pairs={{0,1},{1,2},{2,3},{3,4},{4,5},{5,6},{6,7},{7,8},{8,9},{9,10},{10,1... | collective-permute-start | bytes 2457608 | tf_op jit(solution)/vmap(transpose(jvp()))/dot_general | solution.py:9
  1158.4 28.1 %collective-permute-start.21 = (f32[1,200,1024]{2,1,0:T(8,128)}, f32[1,200,1024]{2,1,0:T(8,128)S(1)}, u32[]{:S(2)}, u32[]{:S(2)}) collective-permute-start(f32[1,200,1024]{2,1,0:T(8,128)} %broadcast_select_fusion.35), channel_id=34, source_target_pairs={{0,15},{1,0},{2,1},{3,2},{4,3},{5,4},{6,5},{7,6},{8,7},{9,8},{10,9... | collective-permute-start | bytes 2457608 | tf_op jit(solution)/vmap(transpose(jvp()))/dot_general | solution.py:9
  1186.8 34.9 %collective-permute-start.22 = (f32[1,200,1024]{2,1,0:T(8,128)S(1)}, f32[1,200,1024]{2,1,0:T(8,128)S(1)}, u32[]{:S(2)}, u32[]{:S(2)}) collective-permute-start(f32[1,200,1024]{2,1,0:T(8,128)S(1)} %get-tuple-element.501), channel_id=37, source_target_pairs={{0,1},{1,2},{2,3},{3,4},{4,5},{5,6},{6,7},{7,8},{8,9},{9,10},{10,1... | collective-permute-start | bytes 2457608 | tf_op jit(solution)/vmap(transpose(jvp()))/dot_general | solution.py:9
  1186.9 34.8 %collective-permute-start.23 = (f32[1,200,1024]{2,1,0:T(8,128)S(1)}, f32[1,200,1024]{2,1,0:T(8,128)S(1)}, u32[]{:S(2)}, u32[]{:S(2)}) collective-permute-start(f32[1,200,1024]{2,1,0:T(8,128)S(1)} %get-tuple-element.502), channel_id=36, source_target_pairs={{0,15},{1,0},{2,1},{3,2},{4,3},{5,4},{6,5},{7,6},{8,7},{9,8},{10,9... | collective-permute-start | bytes 2457608 | tf_op jit(solution)/vmap(transpose(jvp()))/dot_general | solution.py:9
  1224.1 40.8 %collective-permute-start.20 = (f32[1,200,1024]{2,1,0:T(8,128)S(1)}, f32[1,200,1024]{2,1,0:T(8,128)S(1)}, u32[]{:S(2)}, u32[]{:S(2)}) collective-permute-start(f32[1,200,1024]{2,1,0:T(8,128)S(1)} %broadcast_select_fusion.34), channel_id=35, source_target_pairs={{0,1},{1,2},{2,3},{3,4},{4,5},{5,6},{6,7},{7,8},{8,9},{9,10},{10,1... | collective-permute-start | bytes 2457608 | tf_op jit(solution)/vmap(transpose(jvp()))/dot_general | solution.py:9
  1235.4 34.4 %collective-permute-start.21 = (f32[1,200,1024]{2,1,0:T(8,128)}, f32[1,200,1024]{2,1,0:T(8,128)S(1)}, u32[]{:S(2)}, u32[]{:S(2)}) collective-permute-start(f32[1,200,1024]{2,1,0:T(8,128)} %broadcast_select_fusion.35), channel_id=34, source_target_pairs={{0,15},{1,0},{2,1},{3,2},{4,3},{5,4},{6,5},{7,6},{8,7},{9,8},{10,9... | collective-permute-start | bytes 2457608 | tf_op jit(solution)/vmap(transpose(jvp()))/dot_general | solution.py:9
  1270.1 22.7 %collective-permute-start.22 = (f32[1,200,1024]{2,1,0:T(8,128)S(1)}, f32[1,200,1024]{2,1,0:T(8,128)S(1)}, u32[]{:S(2)}, u32[]{:S(2)}) collective-permute-start(f32[1,200,1024]{2,1,0:T(8,128)S(1)} %get-tuple-element.501), channel_id=37, source_target_pairs={{0,1},{1,2},{2,3},{3,4},{4,5},{5,6},{6,7},{7,8},{8,9},{9,10},{10,1... | collective-permute-start | bytes 2457608 | tf_op jit(solution)/vmap(transpose(jvp()))/dot_general | solution.py:9
  1300.8 21.9 %collective-permute-start.20 = (f32[1,200,1024]{2,1,0:T(8,128)S(1)}, f32[1,200,1024]{2,1,0:T(8,128)S(1)}, u32[]{:S(2)}, u32[]{:S(2)}) collective-permute-start(f32[1,200,1024]{2,1,0:T(8,128)S(1)} %broadcast_select_fusion.34), channel_id=35, source_target_pairs={{0,1},{1,2},{2,3},{3,4},{4,5},{5,6},{6,7},{7,8},{8,9},{9,10},{10,1... | collective-permute-start | bytes 2457608 | tf_op jit(solution)/vmap(transpose(jvp()))/dot_general | solution.py:9
  1323.0 22.6 %collective-permute-start.22 = (f32[1,200,1024]{2,1,0:T(8,128)S(1)}, f32[1,200,1024]{2,1,0:T(8,128)S(1)}, u32[]{:S(2)}, u32[]{:S(2)}) collective-permute-start(f32[1,200,1024]{2,1,0:T(8,128)S(1)} %get-tuple-element.501), channel_id=37, source_target_pairs={{0,1},{1,2},{2,3},{3,4},{4,5},{5,6},{6,7},{7,8},{8,9},{9,10},{10,1... | collective-permute-start | bytes 2457608 | tf_op jit(solution)/vmap(transpose(jvp()))/dot_general | solution.py:9
  1323.0 22.5 %collective-permute-start.23 = (f32[1,200,1024]{2,1,0:T(8,128)S(1)}, f32[1,200,1024]{2,1,0:T(8,128)S(1)}, u32[]{:S(2)}, u32[]{:S(2)}) collective-permute-start(f32[1,200,1024]{2,1,0:T(8,128)S(1)} %get-tuple-element.502), channel_id=36, source_target_pairs={{0,15},{1,0},{2,1},{3,2},{4,3},{5,4},{6,5},{7,6},{8,7},{9,8},{10,9... | collective-permute-start | bytes 2457608 | tf_op jit(solution)/vmap(transpose(jvp()))/dot_general | solution.py:9
  1390.5 211.4 %collective-permute-start.29 = (f32[1,200,1024]{2,1,0:T(8,128)}, f32[1,200,1024]{2,1,0:T(8,128)}, u32[]{:S(2)}, u32[]{:S(2)}) collective-permute-start(f32[1,200,1024]{2,1,0:T(8,128)} %get-tuple-element.47), channel_id=38, source_target_pairs={{0,1},{1,2},{2,3},{3,4},{4,5},{5,6},{6,7},{7,8},{8,9},{9,10},{10,1... | collective-permute-start | bytes 2457608 | tf_op jit(solution)/vmap(transpose(jvp()))/dot_general | solution.py:9
  1415.4 21.7 %collective-permute-start.16 = (f32[1,200,1024]{2,1,0:T(8,128)S(1)}, f32[1,200,1024]{2,1,0:T(8,128)S(1)}, u32[]{:S(2)}, u32[]{:S(2)}) collective-permute-start(f32[1,200,1024]{2,1,0:T(8,128)S(1)} %broadcast_select_fusion.32), channel_id=29, source_target_pairs={{0,1},{1,2},{2,3},{3,4},{4,5},{5,6},{6,7},{7,8},{8,9},{9,10},{10,1... | collective-permute-start | bytes 2457608 | tf_op jit(solution)/vmap(transpose(jvp()))/dot_general | solution.py:9
  1438.5 22.6 %collective-permute-start.18 = (f32[1,200,1024]{2,1,0:T(8,128)S(1)}, f32[1,200,1024]{2,1,0:T(8,128)S(1)}, u32[]{:S(2)}, u32[]{:S(2)}) collective-permute-start(f32[1,200,1024]{2,1,0:T(8,128)S(1)} %get-tuple-element.492), channel_id=31, source_target_pairs={{0,1},{1,2},{2,3},{3,4},{4,5},{5,6},{6,7},{7,8},{8,9},{9,10},{10,1... | collective-permute-start | bytes 2457608 | tf_op jit(solution)/vmap(transpose(jvp()))/dot_general | solution.py:9
  1438.6 22.5 %collective-permute-start.19 = (f32[1,200,1024]{2,1,0:T(8,128)S(1)}, f32[1,200,1024]{2,1,0:T(8,128)}, u32[]{:S(2)}, u32[]{:S(2)}) collective-permute-start(f32[1,200,1024]{2,1,0:T(8,128)S(1)} %get-tuple-element.493), channel_id=30, source_target_pairs={{0,15},{1,0},{2,1},{3,2},{4,3},{5,4},{6,5},{7,6},{8,7},{9,8},{10,9... | collective-permute-start | bytes 2457608 | tf_op jit(solution)/vmap(transpose(jvp()))/dot_general | solution.py:9
  1464.6 21.8 %collective-permute-start.16 = (f32[1,200,1024]{2,1,0:T(8,128)S(1)}, f32[1,200,1024]{2,1,0:T(8,128)S(1)}, u32[]{:S(2)}, u32[]{:S(2)}) collective-permute-start(f32[1,200,1024]{2,1,0:T(8,128)S(1)} %broadcast_select_fusion.32), channel_id=29, source_target_pairs={{0,1},{1,2},{2,3},{3,4},{4,5},{5,6},{6,7},{7,8},{8,9},{9,10},{10,1... | collective-permute-start | bytes 2457608 | tf_op jit(solution)/vmap(transpose(jvp()))/dot_general | solution.py:9
  1511.1 21.7 %collective-permute-start.16 = (f32[1,200,1024]{2,1,0:T(8,128)S(1)}, f32[1,200,1024]{2,1,0:T(8,128)S(1)}, u32[]{:S(2)}, u32[]{:S(2)}) collective-permute-start(f32[1,200,1024]{2,1,0:T(8,128)S(1)} %broadcast_select_fusion.32), channel_id=29, source_target_pairs={{0,1},{1,2},{2,3},{3,4},{4,5},{5,6},{6,7},{7,8},{8,9},{9,10},{10,1... | collective-permute-start | bytes 2457608 | tf_op jit(solution)/vmap(transpose(jvp()))/dot_general | solution.py:9
  (161 other events, 3451.4 us)
Sparse Core Ops, SparseCore 0:
  853.8 158.6 all-gather.9
  1132.8 145.5 all-gather.11
  1620.6 102.5 all-gather.13
where the time goes:
time: 1760 us
  waiting for transfers between devices  707 us (40%)
  matrix products  461 us (26%)
  starting transfers between devices  299 us (17%)
  other arithmetic  119 us (7%)
  local copies, waits for them, and re-layouts  106 us (6%)
  loops' own time  49.7 us (3%)
    dot_general x34, waiting for transfers between devices, layer(): up = jnp.dot(a, w['w_up'], preferred_element_type=jnp.float32)  220 us
    dot_general x34, waiting for transfers between devices, matmul(): jnp.dot(a, w, preferred_element_type=jnp.float32).astype(jnp.bfloat16)  219 us
    dot_general x19, matrix products, matmul(): jnp.dot(a, w, preferred_element_type=jnp.float32).astype(jnp.bfloat16)  171 us
    dot_general x34, waiting for transfers between devices, layer(): gate = jnp.dot(a, w['w_gate'], preferred_element_type=jnp.float32)  165 us
    dot_general x19, matrix products, layer(): up = jnp.dot(a, w['w_up'], preferred_element_type=jnp.float32)  155 us
    dot_general x19, matrix products, layer(): gate = jnp.dot(a, w['w_gate'], preferred_element_type=jnp.float32)  135 us
    dot_general x34, starting transfers between devices, layer(): up = jnp.dot(a, w['w_up'], preferred_element_type=jnp.float32)  134 us
    reshape x3, waiting for transfers between devices, step(): t.reshape(-1, *t.shape[2:])  103 us
  transfers between devices with their start and end apart: 105, of which 63 were waited for; matrix products, arithmetic and copies ran while one was open for 21% of the time, Pallas kernels for 0%

commit v1 on v0

v1 whole, which is shorter than its diff:
```python
import functools

import jax
import jax.numpy as jnp
from jax import lax
from jax.experimental import pallas as pl
from jax.experimental.pallas import tpu as pltpu
from jax.sharding import PartitionSpec as P

BF = jnp.bfloat16
F32 = jnp.float32
MESH = pl.DeviceIdType.MESH
NS = 8
NL = 4
LAST = 13


def _pieces(mat, a):
    if mat < 2:
        r = 64 // a
        return [(0, i * r, r, 0, i) for i in range(3)] + [(1, i * r, r, 0, 3 + i) for i in range(2)]
    t = 8 // a
    return [(0, i * 24, 24, 0, i) for i in range(t)] + [(1, i * 16, 16, 24, i) for i in range(t)]


def _dims(mat, a):
    return (64 // a, 640) if mat < 2 else (40, 1024 // a)


def _place(mat, a, s):
    if mat < 2:
        return (s % a) * (64 // a), pl.multiple_of((s // a) * 640, 128)
    return pl.multiple_of((s // a) * 40, 8), pl.multiple_of((s % a) * (1024 // a), 128)


def _cut(mat, a, s, part=None):
    r0, c0 = _place(mat, a, s)
    r, c = _dims(mat, a)
    if part is None:
        return pl.ds(r0, r), pl.ds(c0, c)
    if mat < 2:
        return pl.ds(r0, r), pl.ds(c0 + 384 * part, 256 if part else 384)
    return pl.ds(r0 + 24 * part, 16 if part else 24), pl.ds(c0, c)


def comm_kernel(a, *refs):
    g = (refs[0:3], refs[3:6])
    w, m, v = refs[6:9], refs[9:12], refs[12:15]
    ow, om, ov = refs[15:18], refs[18:21], refs[21:24]
    (own, oth, ry, ryz, rr, ll, mbuf, vbuf, wbuf,
     s_own, s_e, r_e, s_y, r_y, s_zr, r_zr, s_zl, r_zl, s_yz, r_yz, s_ld, s_st,
     s_ar, r_ar, s_al, r_al, s_ay, r_ay, s_br, r_br, s_bl, r_bl, s_by, r_by, s_c, r_c) = _group(refs[24:])
    per = 5 * a
    n = 6 * per
    rep, dp = lax.axis_index("rep"), lax.axis_index("dp")
    c, z, y = dp % 2, (dp // 2) % 4, dp // 8
    yz = y * 4 + z
    core, across, right, left = dp + 1 - 2 * c, dp + 8 - 16 * y, dp + 2, dp - 2

    def far(src, dst, ss, rs, to):
        return pltpu.make_async_remote_copy(src_ref=src, dst_ref=dst, send_sem=ss, recv_sem=rs, device_id=(rep, to), device_id_type=MESH)

    def near(src, dst, sem):
        return pltpu.make_async_copy(src, dst, sem)

    @pl.when(z == 0)
    def _():
        for p in range(2):
            rr[p][...] = jnp.zeros_like(rr[p])

    @pl.when(z == 3)
    def _():
        for p in range(2):
            ll[p][...] = jnp.zeros_like(ll[p])

    barrier = pltpu.get_barrier_semaphore()

    def greet(to):
        pl.semaphore_signal(barrier, inc=1, device_id=(rep, to), device_id_type=MESH)

    greet(core)
    greet(across)
    pl.when(z < 3)(lambda: greet(right))
    pl.when(z > 0)(lambda: greet(left))
    pl.semaphore_wait(barrier, 2 + jnp.where(z < 3, 1, 0) + jnp.where(z > 0, 1, 0))

    def what(k):
        mi = k // per
        return 1 - mi // 3, mi % 3, k % per

    def each(mat, do):
        def one(i):
            do(i)

        for i in range(3):
            pl.when(mat == i)(functools.partial(one, i))

    def stage(slot, st, do):
        k = slot - st
        pl.when((k >= 0) & (k < n))(lambda: do(k, k % NS))

    def fetch(k, q):
        layer, mat, s = what(k)

        def of(i, l):
            r0, c0 = _place(i, a, s)
            for part, d0, rows, s0, col in _pieces(i, a):
                at = (pl.ds(r0 + s0, rows), pl.ds(c0 + col * 128, 128))
                to = (q, slice(None), slice(None), pl.ds(d0, rows))
                near(g[l][i].at[(slice(None), slice(None), c, *at)], own[part].at[to], s_own.at[q, part]).start()
                far(g[l][i].at[(slice(None), slice(None), 1 - c, *at)], oth[part].at[to], s_e.at[q, part], r_e.at[q, part], core).start()

        for l in range(2):
            for i in range(3):
                pl.when((layer == l) & (mat == i))(functools.partial(of, i, l))

    def exchange(q, part):
        return far(own[part].at[q], oth[part].at[q], s_e.at[q, part], r_e.at[q, part], core)

    def f(x):
        return x.astype(F32)

    def y_send(q):
        return far(own[0].at[q, 1 - y], ry.at[q], s_y.at[q], r_y.at[q], across)

    def first(k, q):
        for part in range(2):
            near(own[part].at[q], own[part].at[q], s_own.at[q, part]).wait()
            exchange(q, part).wait_recv()

        def add(d):
            own[0][q, 1 - y, d] = (f(own[0][q, 1 - y, d]) + f(oth[0][q, 1 - y, d])).astype(BF)

        loop(0, 4, add)
        y_send(q).start()

    def line(part, q, d, to_right):
        ss, rs, buf = (s_zr, r_zr, rr) if to_right else (s_zl, r_zl, ll)
        to = right if to_right else left
        if part == 0:
            return far(own[0].at[q, y, d], buf[0].at[q, d], ss.at[part, q, d], rs.at[part, q, d], to)
        return far(own[1].at[q, :, d], buf[1].at[q, d], ss.at[part, q, d], rs.at[part, q, d], to)

    def total(part, q, d, buf):
        if part == 0:
            own[0][q, y, d] = (f(own[0][q, y, d]) + f(oth[0][q, y, d]) + f(ry[q, d]) + f(buf[0][q, d])).astype(BF)
        else:
            for j in range(2):
                own[1][q, j, d] = (f(own[1][q, j, d]) + f(oth[1][q, j, d]) + f(buf[1][q, d, j])).astype(BF)

    def loop(lo, hi, do):
        def one(d, _):
            do(d)
            return 0

        lax.fori_loop(lo, hi, one, 0)

    def go(to_right, part, k, q):
        buf = rr if to_right else ll

        def give(d):
            total(part, q, d, buf)
            line(part, q, d, to_right).start()

        def take(d):
            line(part, q, d, to_right).wait_recv()

        if to_right:
            pl.when(z > 0)(lambda: loop(z, 4, take))
            loop(z + 1, 4, give)
        else:
            pl.when(z < 3)(lambda: loop(0, z + 1, take))
            loop(0, z, give)

    def yz_send(q):
        return far(own[1].at[q, 1 - y, z], ryz.at[q], s_yz.at[q], r_yz.at[q], across)

    def yz(k, q):
        own[1][q, 1 - y, z] = (f(own[1][q, 1 - y, z]) + f(oth[1][q, 1 - y, z]) + f(rr[1][q, z, 1 - y]) + f(ll[1][q, z, 1 - y])).astype(BF)
        yz_send(q).start()

    def small(i, q, k, put):
        return [near(*d) for d in _small(i, q, k, put)]

    def _small(i, q, k, put):
        layer, _, s = what(k)
        rows, cols = _cut(i, a, s)
        x = k % NL
        t = 0 if i < 2 else 1
        if put:
            return [(mbuf[t].at[x], om[i].at[layer, rows, cols], s_st.at[x, 0]),
                    (vbuf[t].at[x], ov[i].at[layer, rows, cols], s_st.at[x, 1]),
                    (wbuf[t].at[x], ow[i].at[layer, y, z, c, rows, cols], s_st.at[x, 2])]
        return [(m[i].at[layer, rows, cols], mbuf[t].at[x], s_ld.at[x, 0]),
                (v[i].at[layer, rows, cols], vbuf[t].at[x], s_ld.at[x, 1]),
                (w[i].at[layer, y, z, c, rows, cols], wbuf[t].at[x], s_ld.at[x, 2])]

    def load(k, q):
        each(what(k)[1], lambda i: [d.start() for d in small(i, q, k, False)])

    def final(k, q):
        yz_send(q).wait_recv()
        x = k % NL

        def of(i):
            for d in small(i, q, k, False):
                d.wait()
            t = 0 if i < 2 else 1
            for part, d0, rows, s0, col in _pieces(i, a):
                at = pl.ds(d0, rows)
                if part == 0:
                    gr = (f(own[0][q, y, z, at]) + f(oth[0][q, y, z, at]) + f(ry[q, z, at])
                          + f(rr[0][q, z, at]) + f(ll[0][q, z, at]))
                else:
                    gr = (f(own[1][q, y, z, at]) + f(oth[1][q, y, z, at]) + f(rr[1][q, z, y, at])
                          + f(ll[1][q, z, y, at]) + f(ryz[q, at]))
                gr = f(gr.astype(BF))
                b = (x, pl.ds(s0, rows), pl.ds(col * 128, 128))
                mm = 0.9 * mbuf[t][b] + 0.1 * gr
                vv = 0.95 * vbuf[t][b] + 0.05 * gr * gr
                ww = f(wbuf[t][b])
                mbuf[t][b] = mm
                vbuf[t][b] = vv
                wbuf[t][b] = (ww - 0.02 * (mm * lax.rsqrt(vv + 1e-8) + 0.1 * ww)).astype(BF)
            for d in small(i, q, k, True):
                d.start()

        each(what(k)[1], of)

    def block(i, k, part, by, bz):
        layer, _, s = what(k)
        rows, cols = _cut(i, a, s, part)
        return ow[i].at[layer, by, bz, c, rows, cols]

    def pair(i, k, bz):
        layer, _, s = what(k)
        rows, cols = _cut(i, a, s, 1)
        return ow[i].at[layer, :, bz, c, rows, cols]

    def same(ref, ss, rs, to):
        return lambda: far(ref, ref, ss, rs, to)

    def moves(i, k, q, t):
        out = []
        b = block(i, k, 0, y, z)
        cs = s_c.at
        if t == 0:
            out.append((None, None, [
                (z < 3, same(b, s_ar.at[q, 0], r_ar.at[q, 0], right)),
                (z > 0, same(b, s_al.at[q, 0], r_al.at[q, 0], left)),
                (None, same(b, s_ay.at[q, 0], r_ay.at[q, 0], across)),
                (None, same(b, cs[q, 0], r_c.at[k % (2 * NS)], core)),
            ]))
            e = block(i, k, 1, y, z)
            out.append((None, None, [
                (None, same(e, s_by.at[q], r_by.at[q], across)),
                (None, same(e, cs[q, 14], r_c.at[k % (2 * NS)], core)),
            ]))
        if 1 <= t <= 3:
            b = block(i, k, 0, y, z - t)
            sends = [(None, same(b, s_ay.at[q, t], r_ay.at[q, t], across)), (None, same(b, cs[q, t], r_c.at[k % (2 * NS)], core))]
            if t < 3:
                sends.insert(0, (z < 3, same(b, s_ar.at[q, t], r_ar.at[q, t], right)))
            out.append((z >= t, same(b, s_ar.at[q, t - 1], r_ar.at[q, t - 1], right), sends))
            b = block(i, k, 0, y, z + t)
            sends = [(None, same(b, s_ay.at[q, 3 + t], r_ay.at[q, 3 + t], across)), (None, same(b, cs[q, 3 + t], r_c.at[k % (2 * NS)], core))]
            if t < 3:
                sends.insert(0, (z > 0, same(b, s_al.at[q, t], r_al.at[q, t], left)))
            out.append((z + t <= 3, same(b, s_al.at[q, t - 1], r_al.at[q, t - 1], left), sends))
        if 1 <= t <= 4:
            u = t - 1
            b = block(i, k, 0, 1 - y, z - u)
            out.append((None if u == 0 else z >= u, same(b, s_ay.at[q, u], r_ay.at[q, u], across), [(None, same(b, cs[q, 7 + u], r_c.at[k % (2 * NS)], core))]))
            if u:
                b = block(i, k, 0, 1 - y, z + u)
                out.append((z + u <= 3, same(b, s_ay.at[q, 3 + u], r_ay.at[q, 3 + u], across), [(None, same(b, cs[q, 10 + u], r_c.at[k % (2 * NS)], core))]))
        if t == 1:
            e, p = block(i, k, 1, 1 - y, z), pair(i, k, z)
            out.append((None, same(e, s_by.at[q], r_by.at[q], across), [
                (z < 3, same(p, s_br.at[q, 0], r_br.at[q, 0], right)),
                (z > 0, same(p, s_bl.at[q, 0], r_bl.at[q, 0], left)),
                (None, same(e, cs[q, 15], r_c.at[k % (2 * NS)], core)),
            ]))
        if 2 <= t <= 4:
            u = t - 1
            p = pair(i, k, z - u)
            sends = [(None, same(p, cs[q, 15 + u], r_c.at[k % (2 * NS)], core))]
            if u < 3:
                sends.insert(0, (z < 3, same(p, s_br.at[q, u], r_br.at[q, u], right)))
            out.append((z >= u, same(p, s_br.at[q, u - 1], r_br.at[q, u - 1], right), sends))
            p = pair(i, k, z + u)
            sends = [(None, same(p, cs[q, 18 + u], r_c.at[k % (2 * NS)], core))]
            if u < 3:
                sends.insert(0, (z > 0, same(p, s_bl.at[q, u], r_bl.at[q, u], left)))
            out.append((z + u <= 3, same(p, s_bl.at[q, u - 1], r_bl.at[q, u - 1], left), sends))
        return out

    def when(cond, do):
        do() if cond is None else pl.when(cond)(lambda: do())

    def spread(t, k, q):
        def of(i):
            if t == 0:
                for d in small(i, q, k, True):
                    d.wait()
            for cond, wait, sends in moves(i, k, q, t):
                def go(wait=wait, sends=sends):
                    if wait is not None:
                        wait().wait_recv()
                    for on, copy in sends:
                        when(on, lambda copy=copy: copy().start())
                when(cond, go)

        each(what(k)[1], of)

    def finish(k, q):
        def of(i):
            layer, _, s = what(k)
            rows, cols = _cut(i, a, s)
            b = ow[i].at[layer, :, :, 1 - c, rows, cols]
            same(b, s_c.at[q, 0], r_c.at[k % (2 * NS)], core)().wait_recv()
            for t in range(5):
                for cond, _, sends in moves(i, k, q, t):
                    def go(sends=sends):
                        for on, copy in sends:
                            when(on, lambda copy=copy: copy().wait_send())
                    when(cond, go)

        each(what(k)[1], of)

    def sent(k, q):
        for part in range(2):
            exchange(q, part).wait_send()

            loop(z + 1, 4, lambda d, part=part: line(part, q, d, True).wait_send())
            loop(0, z, lambda d, part=part: line(part, q, d, False).wait_send())
        y_send(q).wait_send()
        yz_send(q).wait_send()

    def slot(i, _):
        stage(i, 0, fetch)
        stage(i, 1, first)
        stage(i, 2, lambda k, q: y_send(q).wait_recv())
        for part, base in ((1, 1), (0, 2)):
            stage(i, base + z, functools.partial(go, True, part))
            stage(i, base + 3 - z, functools.partial(go, False, part))
        stage(i, 4, yz)
        stage(i, 3, load)
        stage(i, 5, final)
        for t in range(5):
            stage(i, 6 + t, functools.partial(spread, t))
        stage(i, 7, sent)
        stage(i, 12, finish)
        return 0

    lax.fori_loop(0, n + LAST, slot, 0)


def _scratch(a):
    ry, rz = 192 // a, 128 // a
    d = pltpu.SemaphoreType.DMA
    A, B = _dims(0, a), _dims(2, a)
    shapes = [
        [pltpu.VMEM((NS, 2, 4, r, 128), BF) for r in (ry, rz)],
        [pltpu.VMEM((NS, 2, 4, r, 128), BF) for r in (ry, rz)],
        pltpu.VMEM((NS, 4, ry, 128), BF),
        pltpu.VMEM((NS, rz, 128), BF),
        [pltpu.VMEM((NS, 4, ry, 128), BF), pltpu.VMEM((NS, 4, 2, rz, 128), BF)],
        [pltpu.VMEM((NS, 4, ry, 128), BF), pltpu.VMEM((NS, 4, 2, rz, 128), BF)],
        [pltpu.VMEM((NL, *A), F32), pltpu.VMEM((NL, *B), F32)],
        [pltpu.VMEM((NL, *A), F32), pltpu.VMEM((NL, *B), F32)],
        [pltpu.VMEM((NL, *A), BF), pltpu.VMEM((NL, *B), BF)],
        d((NS, 2)), d((NS, 2)), d((NS, 2)), d((NS,)), d((NS,)),
        d((2, NS, 4)), d((2, NS, 4)), d((2, NS, 4)), d((2, NS, 4)), d((NS,)), d((NS,)), d((NL, 3)), d((NL, 3)),
        d((NS, 3)), d((NS, 3)), d((NS, 3)), d((NS, 3)), d((NS, 7)), d((NS, 7)),
        d((NS, 3)), d((NS, 3)), d((NS, 3)), d((NS, 3)), d((NS,)), d((NS,)), d((NS, 22)), d((2 * NS,)),
    ]
    return shapes


def _group(flat):
    like, out, j = _scratch(1), [], 0
    for s in like:
        if isinstance(s, list):
            out.append(flat[j : j + len(s)])
            j += len(s)
        else:
            out.append(flat[j])
            j += 1
    return out


def comm(g0, g1, w, m, v, a=1):
    def blocks(t):
        lead = t.shape[:-2]
        return t.reshape(*lead, 2, 4, 2, t.shape[-2] // 16, t.shape[-1])

    args = [blocks(t) for t in (*g0, *g1, *w)] + [*m, *v]
    outs = [jax.ShapeDtypeStruct(blocks(t).shape, BF) for t in w] + [jax.ShapeDtypeStruct(t.shape, F32) for t in (*m, *v)]
    flat = [x for s in _scratch(a) for x in (s if isinstance(s, list) else [s])]
    new = pl.pallas_call(
        functools.partial(comm_kernel, a),
        out_shape=outs,
        in_specs=[pl.BlockSpec(memory_space=pl.ANY)] * len(args),
        out_specs=[pl.BlockSpec(memory_space=pl.ANY)] * len(outs),
        scratch_shapes=flat,
        compiler_params=pltpu.CompilerParams(collective_id=0, has_side_effects=True, vmem_limit_bytes=60 << 20),
    )(*args)
    return [n.reshape(t.shape) for n, t in zip(new, (*w, *m, *v))]


def dot(a, b, dims, out=F32):
    return lax.dot_general(a, b, (dims, ((), ())), preferred_element_type=F32).astype(out)


def normed(h):
    wide = h.astype(F32)
    scale = lax.rsqrt(jnp.mean(wide**2, -1, keepdims=True) + 1e-6)
    return (wide * scale).astype(BF), scale


def normed_back(h, scale, da):
    wide, da = h.astype(F32), da.astype(F32)
    inner = jnp.mean(wide * da, -1, keepdims=True)
    return (scale * da - wide * (scale * scale * scale * inner)).astype(BF)


def gated(gate, up):
    return (gate * jax.nn.sigmoid(gate) * up).astype(BF)


def gated_back(gate, up, dhid):
    s = jax.nn.sigmoid(gate)
    dhid = dhid.astype(F32)
    dup = dhid * gate * s
    dgate = dhid * up * (s + gate * s * (1 - s))
    return dgate.astype(BF), dup.astype(BF)


def gradients(x, dy, wg, wu, wd):
    a0, s0 = normed(x)
    gate0 = dot(a0, wg[0], ((1,), (0,)))
    up0 = dot(a0, wu[0], ((1,), (0,)))
    hid0 = gated(gate0, up0)
    h1 = x + dot(hid0, wd[0], ((1,), (0,)), BF)
    a1, s1 = normed(h1)
    gate1 = dot(a1, wg[1], ((1,), (0,)))
    up1 = dot(a1, wu[1], ((1,), (0,)))
    hid1 = gated(gate1, up1)
    out = []

    def back(a, gate, up, hid, dout, wg, wu, wd):
        dhid = dot(dout, wd, ((1,), (1,)), BF)
        dwd = dot(hid, dout, ((0,), (0,)), BF)
        dgate, dup = gated_back(gate, up, dhid)
        dwg = dot(a, dgate, ((0,), (0,)), BF)
        dwu = dot(a, dup, ((0,), (0,)), BF)
        return dgate, dup, dwg, dwu, dwd

    dgate, dup, *g1 = back(a1, gate1, up1, hid1, dy, wg[1], wu[1], wd[1])
    da = dot(dgate, wg[1], ((1,), (1,)), BF) + dot(dup, wu[1], ((1,), (1,)), BF)
    dh1 = dy + normed_back(h1, s1, da)
    _, _, *g0 = back(a0, gate0, up0, hid0, dh1, wg[0], wu[0], wd[0])
    return g1, g0


def solution(mesh):
    def step(x, dy, *arrays):
        w, m, v = (arrays[i : i + 3] for i in (0, 3, 6))
        g1, g0 = gradients(x[0], dy[0], *w)
        return tuple(comm(g0, g1, w, m, v, 2))

    one, whole, rows = P(("rep", "dp")), P(), P(None, "dp")
    return jax.shard_map(
        step,
        mesh=mesh,
        in_specs=(one, one) + (whole,) * 3 + (rows,) * 6,
        out_specs=(P("rep"),) * 3 + (P("rep", "dp"),) * 6,
        check_vma=False,
    )
```

time: 1760 us -> 763 us (0.43)
  waiting for transfers between devices: 707 us -> 0 us
  Pallas kernels: 0 us -> 334 us
  starting transfers between devices: 299 us -> 0 us
  other arithmetic: 119 us -> 9.3 us
  matrix products: 461 us -> 364 us
  local copies, waits for them, and re-layouts: 106 us -> 48.5 us
  loops' own time: 49.7 us -> 0 us
    dot_general x102 -> x0, waiting for transfers between devices: 604 us -> none  [the longest x34 220 us: layer(): up = jnp.dot(a, w['w_up'], preferred_element_type=jnp.float32)]
    pallas_call x0 -> x1, Pallas kernels: none -> 334 us  [comm(): pl.pallas_call(functools.partial(comm_kernel, a), out_shape=outs, in_spec...]
    dot_general x102 -> x0, starting transfers between devices: 299 us -> none  [the longest x34 134 us: layer(): up = jnp.dot(a, w['w_up'], preferred_element_type=jnp.float32)]
    reshape x3 -> x0, waiting for transfers between devices: 103 us -> none  [step(): t.reshape(-1, *t.shape[2:])]
    dot_general x57 -> x15, matrix products: 461 us -> 364 us  [dot(): lax.dot_general(a, b, (dims, ((), ())), preferred_element_type=F32)]
    dot_general x112 -> x0, other arithmetic: 82.8 us -> none
    another operation x6 -> x0, loops' own time: 49.7 us -> none  [the longest x2 17.2 us: layer(): up = jnp.dot(a, w['w_up'], preferred_element_type=jnp.float32)]
    unnamed x57, local copies, waits for them, and re-layouts: 89.9 us -> 48.5 us
  transfers between devices with their start and end apart: 105 -> 0, of which waited for: 63 -> 0; matrix products, arithmetic and copies ran while one was open for 21% -> 0% of each run, Pallas kernels for 0% -> 0%
where the time goes in v1:
time: 763 us; the launch traced here: 757 us
  matrix products  364 us (48%)
  Pallas kernels  334 us (44%)
  local copies, waits for them, and re-layouts  48.5 us (6%)
  other arithmetic  9.3 us (1%)
    dot_general x15, matrix products, dot(): lax.dot_general(a, b, (dims, ((), ())), preferred_element_type=F32)  364 us
    pallas_call x1, Pallas kernels, comm(): pl.pallas_call(functools.partial(comm_kernel, a), out_shape=outs, in_spec...  334 us
    unnamed x57, local copies, waits for them, and re-layouts  48.5 us

profile of v1, /device:TPU:0, one launch (start us, length us, event | category | flops | bytes accessed | tf_op | source)
XLA Modules:
  0.0 756.6 jit_solution(3696435702568047172)
XLA Ops:
  0.6 6.5 copy.20
  7.1 3.1 fusion.18
  10.2 0.0 copy-start.13
  10.2 21.9 %fusion.46 = f32[2048,3200]{1,0:T(8,128)} fusion(bf16[2,1024,3200]{2,1,0:T(8,128)(2,1)} %param.13, bf16[1,2048,1024]{2,1,0:T(8,128)(2,1)} %param.11, f32[2048]{0:T(1024)S(1)} %add_rsqrt_fusion.1), kind=kOutput, calls=%fused_computation.59 | convolution fusion | flops 13428064256 | bytes 36970496 | tf_op jit(solution)/shard_map/dot_general | solution.py:413
  32.1 0.0 copy-done.13
  32.1 32.1 %multiply_convert_fusion.1 = (bf16[2048,3200]{1,0:T(8,128)(2,1)}, f32[2048,3200]{1,0:T(8,128)}) fusion(f32[2048,3200]{1,0:T(8,128)} %fusion.46, bf16[2,1024,3200]{2,1,0:T(8,128)(2,1)} %param.14, bf16[1,2048,1024]{2,1,0:T(8,128)(2,1)} %param.11, f32[2048]{0:T(1024)S(1)} %add_rsqrt_fusion.1), kind=kOutput, calls=%fused_computation.14 | convolution fusion | flops 13467385856 | bytes 76292096 | tf_op jit(solution)/shard_map/dot_general | solution.py:413
  64.2 22.3 %fusion.22 = (f32[2048]{0:T(1024)S(1)}, bf16[2048,1024]{0,1:T(8,128)(2,1)}) fusion(bf16[2048,3200]{1,0:T(8,128)(2,1)} %get-tuple-element.29, bf16[2,3200,1024]{2,1,0:T(8,128)(2,1)} %param.15, bf16[1,2048,1024]{1,2,0:T(8,128)(2,1)} %copy.20), kind=kOutput, calls=%fused_computation.35 | convolution fusion | flops 13432256512 | bytes 28057600 | tf_op jit(solution)/shard_map/dot_general | solution.py:413
  86.5 0.6 copy-done.11
  87.1 23.1 %fusion.38 = f32[2048,3200]{1,0:T(8,128)} fusion(bf16[2,1024,3200]{2,1,0:T(8,128)(2,1)} %param.14, bf16[2048,1024]{0,1:T(8,128)(2,1)} %get-tuple-element.32, f32[2048]{0:T(1024)S(1)} %add_rsqrt_fusion), kind=kOutput, calls=%fused_computation.51 | convolution fusion | flops 13428064256 | bytes 36970496 | tf_op jit(solution)/shard_map/dot_general | solution.py:413
  110.3 0.0 copy-done.4
  110.3 19.5 %convolution_convert_fusion.1 = bf16[2048,3200]{1,0:T(8,128)(2,1)} fusion(bf16[2,3200,1024]{2,1,0:T(8,128)(2,1)} %param.15, bf16[1,2048,1024]{2,1,0:T(8,128)(2,1)S(1)} %copy-done.4), kind=kOutput, calls=%fused_computation.17 | convolution fusion | flops 13428326400 | bytes 23855104 | tf_op jit(solution)/shard_map/dot_general | solution.py:413
  129.8 42.3 %fusion.3 = (bf16[2048,3200]{1,0:T(8,128)(2,1)}, bf16[2048,3200]{1,0:T(8,128)(2,1)}, f32[2048,3200]{1,0:T(8,128)}) fusion(bf16[2048,3200]{1,0:T(8,128)(2,1)} %convolution_convert_fusion.1, f32[2048,3200]{1,0:T(8,128)} %fusion.38, bf16[2,1024,3200]{2,1,0:T(8,128)(2,1)} %param.13, bf16[2048,1024]{0,1:T(8,128)(2,1)} %get-tuple-element.32, ...), kind=kOutput, calls=%fused_computation.7 | convolution fusion | flops 13519814656 | bytes 102506496 | tf_op jit(solution)/shard_map/dot_general | solution.py:413
  172.1 25.7 %fusion.31 = bf16[3200,1024]{1,0:T(8,128)(2,1)} fusion(f32[2048,3200]{1,0:T(8,128)} %fusion.38, f32[2048,3200]{1,0:T(8,128)} %get-tuple-element.33, bf16[1,2048,1024]{2,1,0:T(8,128)(2,1)} %param.12), kind=kOutput, calls=%fused_computation.41 | convolution fusion | flops 13464371200 | bytes 63176704 | tf_op jit(solution)/shard_map/dot_general | solution.py:413
  197.8 21.6 %convolution_convert_fusion.2 = bf16[1024,3200]{1,0:T(8,128)(2,1)} fusion(bf16[2048,3200]{1,0:T(8,128)(2,1)} %get-tuple-element.27, bf16[2048,1024]{0,1:T(8,128)(2,1)} %get-tuple-element.32, f32[2048]{0:T(1024)S(1)} %add_rsqrt_fusion), kind=kOutput, calls=%fused_computation.42 | convolution fusion | flops 13431341056 | bytes 23863296 | tf_op jit(solution)/shard_map/dot_general | solution.py:413
  219.5 0.0 copy-done.2
  219.5 20.3 %convolution_convert_fusion.3 = bf16[1024,3200]{1,0:T(8,128)(2,1)} fusion(bf16[2048,3200]{1,0:T(8,128)(2,1)} %get-tuple-element.28, bf16[2048,1024]{0,1:T(8,128)(2,1)S(1)} %copy-done.2, f32[2048]{0:T(1024)S(1)} %add_rsqrt_fusion), kind=kOutput, calls=%fused_computation.43 | convolution fusion | flops 13431341056 | bytes 23863296 | tf_op jit(solution)/shard_map/dot_general | solution.py:413
  239.8 0.0 slice-done.4
  239.8 0.0 slice-done.5
  239.8 0.0 slice-done.6
  239.8 0.0 slice-done.7
  239.9 17.8 %fusion.32 = bf16[2048,1024]{0,1:T(8,128)(2,1)} fusion(bf16[2048,3200]{1,0:T(8,128)(2,1)} %get-tuple-element.28, bf16[2,1024,3200]{2,1,0:T(8,128)(2,1)S(1)} %bitcast.83), kind=kOutput, calls=%fused_computation.45 | convolution fusion | flops 13421772800 | bytes 23855104 | tf_op jit(solution)/shard_map/dot_general | solution.py:413
  257.7 21.7 %fusion.24 = (f32[2048]{0:T(1024)S(1)}, bf16[2048,1024]{0,1:T(8,128)(2,1)}) fusion(bf16[2048,1024]{0,1:T(8,128)(2,1)S(1)} %copy-done.2, bf16[2048,1024]{0,1:T(8,128)(2,1)} %fusion.32, bf16[2048,3200]{1,0:T(8,128)(2,1)} %get-tuple-element.27, bf16[2,1024,3200]{2,1,0:T(8,128)(2,1)} %param.14), kind=kOutput, calls=%fused_computation.37 | convolution fusion | flops 13434353664 | bytes 32251904 | tf_op jit(solution)/shard_map/dot_general | solution.py:413
  279.4 0.0 copy-done.12
  279.4 6.4 copy.21
  285.9 6.2 fusion.58
  292.1 0.0 copy-start.3
  292.1 20.8 %convolution_convert_fusion.4 = bf16[3200,1024]{1,0:T(8,128)(2,1)} fusion(bf16[2048,3200]{1,0:T(8,128)(2,1)} %get-tuple-element.29, bf16[2048,1024]{0,1:T(8,128)(2,1)S(1)} %fusion.58), kind=kOutput, calls=%fused_computation.44 | convolution fusion | flops 13425049600 | bytes 23855104 | tf_op jit(solution)/shard_map/dot_general | solution.py:413
  312.9 0.0 copy-done.3
  312.9 21.3 %convolution_convert_fusion = bf16[2048,3200]{1,0:T(8,128)(2,1)} fusion(bf16[2048,1024]{0,1:T(8,128)(2,1)} %copy-done.3, bf16[2,3200,1024]{2,1,0:T(8,128)(2,1)} %param.15), kind=kOutput, calls=%fused_computation.16 | convolution fusion | flops 13428326400 | bytes 23855104 | tf_op jit(solution)/shard_map/dot_general | solution.py:413
  334.2 24.1 %fusion.28 = bf16[1024,3200]{1,0:T(8,128)(2,1)} fusion(f32[2048,3200]{1,0:T(8,128)} %fusion.46, bf16[2048,3200]{1,0:T(8,128)(2,1)} %convolution_convert_fusion, bf16[1,2048,1024]{1,2,0:T(8,128)(2,1)S(1)} %copy-done, f32[2048]{0:T(1024)S(1)} %copy-done.14), kind=kOutput, calls=%fused_computation.40 | convolution fusion | flops 13477216256 | bytes 50077696 | tf_op jit(solution)/shard_map/dot_general | solution.py:413
  358.3 29.4 %fusion.25 = bf16[1024,3200]{1,0:T(8,128)(2,1)} fusion(f32[2048,3200]{1,0:T(8,128)} %get-tuple-element.30, bf16[2048,3200]{1,0:T(8,128)(2,1)} %convolution_convert_fusion, f32[2048,3200]{1,0:T(8,128)} %fusion.46, bf16[1,2048,1024]{1,2,0:T(8,128)(2,1)S(1)} %copy-done, f32[2048]{0:T(1024)S(1)} %copy-done.14), kind=kOutput, calls=%fused_computation.39 | convolution fusion | flops 13503430656 | bytes 76292096 | tf_op jit(solution)/shard_map/dot_general | solution.py:413
  387.6 333.9 %shard_map.178 = (bf16[2,2,4,2,64,3200]{5,4,3,2,1,0:T(8,128)(2,1)}, bf16[2,2,4,2,64,3200]{5,4,3,2,1,0:T(8,128)(2,1)}, bf16[2,2,4,2,200,1024]{5,4,3,2,1,0:T(8,128...) custom-call(bf16[2,4,2,64,3200]{4,3,2,1,0:T(8,128)(2,1)} %bitcast.91, ...), custom_call_target="tpu_custom_call" | custom-call | tf_op jit(solution)/shard_map/pallas_call | solution.py:401
  721.6 0.0 slice-start
  721.6 0.0 slice-start.1
  721.6 12.7 %copy.31 = bf16[2,1024,3200]{2,1,0:T(8,128)(2,1)} copy(bf16[2,1024,3200]{2,1,0:T(8,128)(2,1)} %bitcast.80) | data formatting | bytes 26214400
  734.3 6.6 copy.32
  740.9 1.2 slice-done.1
  742.1 1.3 slice-done.2
  743.3 0.0 slice-done.3
  743.4 6.1 copy.33
  749.5 1.2 copy.34
  750.7 1.2 copy.35
  751.8 0.0 copy-done.8
  751.8 1.2 copy.36
  753.0 1.2 copy.37
  754.2 0.0 copy-done.6
  754.2 1.2 copy.38
  755.3 1.2 copy.39
  (32 shorter events, 0.1 us)
Async XLA Ops:
  10.2 21.9 %copy-start.13 = (f32[2048]{0:T(1024)}, f32[2048]{0:T(1024)S(1)}, u32[]{:S(2)}) copy-start(f32[2048]{0:T(1024)S(1)} %add_rsqrt_fusion.1) | copy-start | bytes 24580
  86.5 0.6 copy-start.11
  87.1 23.1 %copy-start.4 = (bf16[1,2048,1024]{2,1,0:T(8,128)(2,1)S(1)}, bf16[1,2048,1024]{2,1,0:T(8,128)(2,1)}, u32[]{:S(2)}) copy-start(bf16[1,2048,1024]{2,1,0:T(8,128)(2,1)} %param.12) | copy-start | bytes 12582916
  197.8 21.6 %copy-start.2 = (bf16[2048,1024]{0,1:T(8,128)(2,1)S(1)}, bf16[2048,1024]{0,1:T(8,128)(2,1)}, u32[]{:S(2)}) copy-start(bf16[2048,1024]{0,1:T(8,128)(2,1)} %get-tuple-element.32) | copy-start | bytes 12582916
  197.8 42.0 %slice-start.4 = ((s8[13107200]{0:T(1024)(128)(4,1)}), s8[4194304]{0:T(1024)(128)(4,1)S(1)}, s32[]{:S(2)}) async-start(s8[13107200]{0:T(1024)(128)(4,1)} %bitcast.82), calls=%async_computation.4 | async-start | bytes 8388608
  197.8 42.0 %slice-start.5 = ((s8[13107200]{0:T(1024)(128)(4,1)}), s8[4194304]{0:T(1024)(128)(4,1)S(1)}, s32[]{:S(2)}) async-start(s8[13107200]{0:T(1024)(128)(4,1)} %bitcast.82), calls=%async_computation.5 | async-start | bytes 8388608
  219.5 20.4 %slice-start.6 = ((s8[13107200]{0:T(1024)(128)(4,1)}), s8[4194304]{0:T(1024)(128)(4,1)S(1)}, s32[]{:S(2)}) async-start(s8[13107200]{0:T(1024)(128)(4,1)} %bitcast.82), calls=%async_computation.6 | async-start | bytes 8388608
  219.5 20.4 %slice-start.7 = ((s8[13107200]{0:T(1024)(128)(4,1)}), s8[524288]{0:T(1024)(128)(4,1)S(1)}, s32[]{:S(2)}) async-start(s8[13107200]{0:T(1024)(128)(4,1)} %bitcast.82), calls=%async_computation.7 | async-start | bytes 1048576
  257.7 21.7 %copy-start.12 = (f32[2048]{0:T(1024)S(1)}, f32[2048]{0:T(1024)}, u32[]{:S(2)}) copy-start(f32[2048]{0:T(1024)} %copy-done.11) | copy-start | bytes 24580
  292.1 20.8 %copy-start.3 = (bf16[2048,1024]{0,1:T(8,128)(2,1)}, bf16[2048,1024]{0,1:T(8,128)(2,1)S(1)}, u32[]{:S(2)}) copy-start(bf16[2048,1024]{0,1:T(8,128)(2,1)S(1)} %fusion.58) | copy-start | bytes 12582916
  312.9 21.3 %copy-start = (bf16[1,2048,1024]{1,2,0:T(8,128)(2,1)S(1)}, bf16[1,2048,1024]{1,2,0:T(8,128)(2,1)}, u32[]{:S(2)}) copy-start(bf16[1,2048,1024]{1,2,0:T(8,128)(2,1)} %copy.20) | copy-start | bytes 12582916
  312.9 21.3 %copy-start.14 = (f32[2048]{0:T(1024)S(1)}, f32[2048]{0:T(1024)}, u32[]{:S(2)}) copy-start(f32[2048]{0:T(1024)} %copy-done.13) | copy-start | bytes 24580
  721.5 12.7 %copy-start.1 = (bf16[2,2,4,2,64,3200]{5,4,3,2,1,0:T(8,128)(2,1)S(1)}, bf16[2,2,4,2,64,3200]{5,4,3,2,1,0:T(8,128)(2,1)}, u32[]{:S(2)}) copy-start(bf16[2,2,4,2,64,3200]{5,4,3,2,1,0:T(8,128)(2,1)} %get-tuple-element.19) | copy-start | bytes 39321604
  721.6 19.4 %slice-start = ((s8[13107200]{0:T(1024)(128)(4,1)}), s8[4194304]{0:T(1024)(128)(4,1)S(1)}, s32[]{:S(2)}) async-start(s8[13107200]{0:T(1024)(128)(4,1)} %bitcast.76), calls=%async_computation | async-start | bytes 8388608
  721.6 20.5 %slice-start.1 = ((s8[13107200]{0:T(1024)(128)(4,1)}), s8[4194304]{0:T(1024)(128)(4,1)S(1)}, s32[]{:S(2)}) async-start(s8[13107200]{0:T(1024)(128)(4,1)} %bitcast.76), calls=%async_computation.1 | async-start | bytes 8388608
  734.3 9.1 %slice-start.2 = ((s8[13107200]{0:T(1024)(128)(4,1)}), s8[4194304]{0:T(1024)(128)(4,1)S(1)}, s32[]{:S(2)}) async-start(s8[13107200]{0:T(1024)(128)(4,1)} %bitcast.76), calls=%async_computation.2 | async-start | bytes 8388608
  734.3 9.1 %slice-start.3 = ((s8[13107200]{0:T(1024)(128)(4,1)}), s8[524288]{0:T(1024)(128)(4,1)S(1)}, s32[]{:S(2)}) async-start(s8[13107200]{0:T(1024)(128)(4,1)} %bitcast.76), calls=%async_computation.3 | async-start | bytes 1048576
  743.4 6.1 copy-start.10
  743.4 7.3 copy-start.9
  743.4 8.5 %copy-start.8 = (f32[2,200,1024]{2,1,0:T(8,128)S(1)}, f32[2,200,1024]{2,1,0:T(8,128)}, u32[]{:S(2)}) copy-start(f32[2,200,1024]{2,1,0:T(8,128)} %get-tuple-element.50) | copy-start | bytes 4915204
  749.5 3.5 copy-start.7
  749.5 4.7 copy-start.6
  749.5 5.8 copy-start.5

commit v2 on v0

v2 whole, which is shorter than its diff:
```python
import functools

import jax
import jax.numpy as jnp
from jax import lax
from jax.experimental import pallas as pl
from jax.experimental.pallas import tpu as pltpu
from jax.sharding import PartitionSpec as P

BF, F32 = jnp.bfloat16, jnp.float32
MESH = pl.DeviceIdType.MESH
ALL = slice(None)
T, D, F, FB, LANES = 2048, 1024, 3200, 640, 128
BLOCKS = F // FB
TT, TILES = 512, 4
HALF = T // 2
LINE = 4
NS = 8
NL, NW = 4, 16
LAST = 11
LEAD = 3
GATE, UP, DOWN = range(3)
SHAPE = {GATE: (32, FB), UP: (32, FB), DOWN: (40, 512)}
FIRST = {GATE: (32, 384), UP: (32, 384), DOWN: (24, 512)}
MANY = 2
ROWS = (96, 64)
NGU, ND = 20, 10
N = 2 * (NGU + ND)
DA, LOW = 4 * BLOCKS, 4 * BLOCKS + 2 * BLOCKS
END = LOW + 4 * BLOCKS


def _dot(p, q, cp, cq):
    return lax.dot_general(p, q, (((cp,), (cq,)), ((), ())), preferred_element_type=F32)


def f(x):
    return x.astype(F32)


def near(src, dst, sem):
    return pltpu.make_async_copy(src, dst, sem)


def at(k, size):
    return pl.ds(pl.multiple_of(k * size, size), size)


def loop(lo, hi, do):
    def one(d, _):
        do(d)
        return 0

    lax.fori_loop(lo, hi, one, 0)


def run(copies):
    for c in copies:
        c.start()


def wait(copies):
    for c in copies:
        c.wait()


def pieces(kind):
    (r, c), (r0, c0) = SHAPE[kind], FIRST[kind]
    if kind < DOWN:
        left = c0 // LANES
        return [(0, i * r, r, 0, i) for i in range(left)] + [(1, (i - left) * r, r, 0, i) for i in range(left, c // LANES)]
    return [(p, i * k, k, o, i) for p, k, o in ((0, r0, 0), (1, r - r0, r0)) for i in range(c // LANES)]


def cut(kind, s, part=None):
    (r, c), (r0, c0) = SHAPE[kind], FIRST[kind]
    row, col = (s % MANY, s // MANY) if kind < DOWN else (s // MANY, s % MANY)
    row, col = pl.multiple_of(row * r, 8), pl.multiple_of(col * c, LANES)
    if part is None:
        return pl.ds(row, r), pl.ds(col, c)
    if kind < DOWN:
        return pl.ds(row, r), pl.ds(col + c0, c - c0) if part else pl.ds(col, c0)
    return pl.ds(row + r0, r - r0) if part else pl.ds(row, r0), pl.ds(col, c)


def step_kernel(*refs):
    refs = list(refs)

    def take(n):
        out = refs[:n]
        del refs[:n]
        return out

    x, dy = take(2)
    nat, w, m, v, ow, om, ov, g = (take(3) for _ in range(8))
    dgu_all, gate0, up0, a0, h1 = take(5)
    own, oth, rr, ll, mbuf, vbuf, wbuf = (take(2) for _ in range(7))
    (ry, ryz, s_own, s_e, r_e, s_y, r_y, s_zr, r_zr, s_zl, r_zl, s_yz, r_yz, s_ld, s_st,
     s_ar, r_ar, s_al, r_al, s_ay, r_ay, s_br, r_br, s_bl, r_bl, s_by, r_by, s_c, r_c,
     av, dv, wgu, wd, hid, dgu, gout, dout, acc, gt,
     s_x, s_dy, s_w, s_wd, s_dgu, s_go, s_do, s_dl, s_gt, s_h, s_a0, s_keep, s_h1) = refs
    rep, dp = lax.axis_index("rep"), lax.axis_index("dp")
    c, z, y = dp % 2, (dp // 2) % LINE, dp // (2 * LINE)
    core, across, right, left = dp + 1 - 2 * c, dp + (1 - 2 * y) * 2 * LINE, dp + 2, dp - 2
    more, less = z < LINE - 1, z > 0

    def far(src, dst, ss, rs, to):
        return pltpu.make_async_remote_copy(src_ref=src, dst_ref=dst, send_sem=ss, recv_sem=rs, device_id=(rep, to), device_id_type=MESH)

    def clear(bufs):
        for b in bufs:
            b[...] = jnp.zeros_like(b)

    pl.when(z == 0)(lambda: clear(rr))
    pl.when(z == LINE - 1)(lambda: clear(ll))
    barrier = pltpu.get_barrier_semaphore()

    def greet(to):
        pl.semaphore_signal(barrier, inc=1, device_id=(rep, to), device_id_type=MESH)

    greet(core)
    greet(across)
    pl.when(more)(lambda: greet(right))
    pl.when(less)(lambda: greet(left))
    def what(k):
        u = k % (NGU + ND)
        gu = u < NGU
        return 1 - k // (NGU + ND), jnp.where(gu, (u // 2) % 2, DOWN), jnp.where(gu, (u // 4) * 2 + u % 2, u - NGU)

    def each(kind, do):
        def one(i):
            do(i)

        for i in SHAPE:
            pl.when(kind == i)(functools.partial(one, i))

    def stage(tick, st, do):
        k = tick - st
        pl.when((k >= 0) & (k < N))(lambda: do(k, k % NS))

    def fetch(k, q):
        layer, kind, s = what(k)

        def of(i):
            rows, cols = cut(i, s)
            for part, d0, n, s0, col in pieces(i):
                cc = pl.ds(cols.start + col * LANES, LANES)
                here = (pl.ds(rows.start + s0, n), cc) if i < DOWN else (s // MANY, pl.ds(s0, n), cc)
                to = (q, ALL, ALL, pl.ds(d0, n))
                mine, other = ((layer, ALL, ALL, h, *here) for h in (c, 1 - c))
                src = g[i]
                near(src.at[mine], own[part].at[to], s_own.at[q, part]).start()
                far(src.at[other], oth[part].at[to], s_e.at[q, part], r_e.at[q, part], core).start()

        each(kind, of)

    def exchange(q, part):
        return far(own[part].at[q], oth[part].at[q], s_e.at[q, part], r_e.at[q, part], core)

    def y_send(q):
        return far(own[0].at[q, 1 - y], ry.at[q], s_y.at[q], r_y.at[q], across)

    def first(k, q):
        for part in range(2):
            near(own[part].at[q], own[part].at[q], s_own.at[q, part]).wait()
            exchange(q, part).wait_recv()

        def add(d):
            own[0][q, 1 - y, d] = (f(own[0][q, 1 - y, d]) + f(oth[0][q, 1 - y, d])).astype(BF)

        loop(0, LINE, add)
        y_send(q).start()

    def line(part, q, d, to_right):
        ss, rs, buf, to = (s_zr, r_zr, rr, right) if to_right else (s_zl, r_zl, ll, left)
        src = own[0].at[q, y, d] if part == 0 else own[1].at[q, :, d]
        return far(src, buf[part].at[q, d], ss.at[part, q, d], rs.at[part, q, d], to)

    def total(part, q, d, buf):
        if part == 0:
            own[0][q, y, d] = (f(own[0][q, y, d]) + f(oth[0][q, y, d]) + f(ry[q, d]) + f(buf[0][q, d])).astype(BF)
        else:
            for j in range(2):
                own[1][q, j, d] = (f(own[1][q, j, d]) + f(oth[1][q, j, d]) + f(buf[1][q, d, j])).astype(BF)

    def go(to_right, part, k, q):
        def get(d):
            line(part, q, d, to_right).wait_recv()

        def give(d):
            total(part, q, d, rr if to_right else ll)
            line(part, q, d, to_right).start()

        if to_right:
            pl.when(less)(lambda: loop(z, LINE, get))
            loop(z + 1, LINE, give)
        else:
            pl.when(more)(lambda: loop(0, z + 1, get))
            loop(0, z, give)

    def yz_send(q):
        return far(own[1].at[q, 1 - y, z], ryz.at[q], s_yz.at[q], r_yz.at[q], across)

    def yz(k, q):
        b, r = (q, 1 - y, z), (q, z, 1 - y)
        own[1][b] = (f(own[1][b]) + f(oth[1][b]) + f(rr[1][r]) + f(ll[1][r])).astype(BF)
        yz_send(q).start()

    def small(i, k, put):
        layer, _, s = what(k)
        rows, cols = cut(i, s)
        e, t = k % NL, i // DOWN
        block = (layer, y, z, c, rows, cols)
        there = ((om if put else m)[i].at[layer, rows, cols], (ov if put else v)[i].at[layer, rows, cols], (ow if put else w)[i].at[block])
        here = (mbuf[t].at[e], vbuf[t].at[e], wbuf[t].at[k % NW])
        sems = s_st if put else s_ld
        return [near(b, r, sems.at[e, h]) if put else near(r, b, sems.at[e, h]) for h, (r, b) in enumerate(zip(there, here, strict=True))]

    def final(k, q):
        yz_send(q).wait_recv()

        def of(i):
            wait(small(i, k, False))
            mb, vb, wb = (b[i // DOWN] for b in (mbuf, vbuf, wbuf))
            for part, d0, n, s0, col in pieces(i):
                r = pl.ds(d0, n)
                gr = f(own[part][q, y, z, r]) + f(oth[part][q, y, z, r])
                gr += f(ry[q, z, r]) + f(rr[0][q, z, r]) + f(ll[0][q, z, r]) if part == 0 else f(rr[1][q, z, y, r]) + f(ll[1][q, z, y, r]) + f(ryz[q, r])
                gr = f(gr.astype(BF))
                b = (pl.ds(s0, n), pl.ds(col * LANES, LANES))
                bm, bw = (k % NL, *b), (k % NW, *b)
                mm = 0.9 * mb[bm] + 0.1 * gr
                vv = 0.95 * vb[bm] + 0.05 * gr * gr
                ww = f(wb[bw])
                mb[bm] = mm
                vb[bm] = vv
                wb[bw] = (ww - 0.02 * (mm * lax.rsqrt(vv + 1e-8) + 0.1 * ww)).astype(BF)
            run(small(i, k, True))

        each(what(k)[1], of)
        spread(0, k, q)

    def moves(i, k, q, t):
        layer, _, s = what(k)
        dst = ow[i]

        def block(part, by, bz):
            return dst.at[(layer, by, bz, c, *cut(i, s, part))]

        def mine(part):
            r, cc = SHAPE[i][0] if i < DOWN else FIRST[i][0], FIRST[i][1]
            if part:
                r, cc = (pl.ds(0, r), pl.ds(cc, FB - cc)) if i < DOWN else (pl.ds(r, SHAPE[i][0] - r), pl.ds(0, cc))
            else:
                r, cc = pl.ds(0, r), pl.ds(0, cc)
            return wbuf[i // DOWN].at[k % NW, r, cc]

        def same(ref, ss, rs, n, to, src=None):
            n = q if n is None else (q, n)
            return lambda: far(ref if src is None else src, ref, ss.at[n], rs.at[n], to)

        def along(part, b, n, src=None):
            sr, gr, sl, gl_ = (s_ar, r_ar, s_al, r_al) if part == 0 else (s_br, r_br, s_bl, r_bl)
            return same(b, sr, gr, n, right, src), same(b, sl, gl_, n, left, src)

        out = []
        side = LINE - 1
        b, e = block(0, y, z), block(1, y, z)
        if t == 0:
            r, l = along(0, b, 0, mine(0))
            out.append((None, None, [(more, r), (less, l), (None, same(b, s_ay, r_ay, 0, across, mine(0))), (None, same(e, s_by, r_by, None, across, mine(1)))]))
        elif t <= side:
            for sign, on in ((-1, z >= t), (1, z + t <= side)):
                b = block(0, y, z + sign * t)
                to = 0 if sign < 0 else 1
                sends = [(None, same(b, s_ay, r_ay, t if sign < 0 else side + t, across))]
                if t < side:
                    sends.insert(0, ((more, less)[to], along(0, b, t)[to]))
                out.append((on, along(0, b, t - 1)[to], sends))
        u = t - 1
        if u >= 0:
            for sign, on in ((-1, z >= u), (1, z + u <= side))[: 1 if u == 0 else 2]:
                b = block(0, 1 - y, z + sign * u)
                out.append((on, same(b, s_ay, r_ay, u if sign < 0 else side + u, across), []))
        if u == 0:
            r, l = along(1, dst.at[(layer, ALL, z, c, *cut(i, s, 1))], 0)
            out.append((None, same(e, s_by, r_by, None, across), [(more, r), (less, l)]))
        elif u > 0:
            for sign, on in ((-1, z >= u), (1, z + u <= side)):
                b = dst.at[(layer, ALL, z + sign * u, c, *cut(i, s, 1))]
                to = 0 if sign < 0 else 1
                out.append((on, along(1, b, u - 1)[to], [((more, less)[to], along(1, b, u)[to])] if u < side else []))
        return out

    def when(cond, do):
        do() if cond is None else pl.when(cond)(lambda: do())

    def spread(t, k, q):
        def of(i):
            if t == 1:
                wait(small(i, k, True))
            for cond, first_, sends in moves(i, k, q, t):

                def act(first_=first_, sends=sends):
                    if first_ is not None:
                        first_().wait_recv()
                    for on, copy in sends:
                        when(on, lambda copy=copy: copy().start())

                when(cond, act)

        each(what(k)[1], of)

    def over(i, k, q):
        layer, _, s = what(k)
        b = ow[i].at[(layer, ALL, ALL, c, *cut(i, s))]
        return far(b, b, s_c.at[q], r_c.at[k % (2 * NS)], core)

    def hand(k, q):
        each(what(k)[1], lambda i: over(i, k, q).start())

    def finish(k, q):
        def of(i):
            over(i, k, q).wait()
            for t in range(LINE + 1):
                for cond, _, sends in moves(i, k, q, t):

                    def act(sends=sends):
                        for on, copy in sends:
                            when(on, lambda copy=copy: copy().wait_send())

                    if sends:
                        when(cond, act)

        each(what(k)[1], of)

    def sent(k, q):
        for part in range(2):
            exchange(q, part).wait_send()
            loop(z + 1, LINE, lambda d, part=part: line(part, q, d, True).wait_send())
            loop(0, z, lambda d, part=part: line(part, q, d, False).wait_send())
        y_send(q).wait_send()
        yz_send(q).wait_send()

    def communicate(i):
        stage(i, 0, first)
        stage(i, 1, lambda k, q: y_send(q).wait_recv())
        for part in (1, 0):
            base = 1 - part
            stage(i, base + z, functools.partial(go, True, part))
            stage(i, base + LINE - 1 - z, functools.partial(go, False, part))
        stage(i, LINE - 1, yz)
        stage(i, LINE - 2, lambda k, q: each(what(k)[1], lambda e: run(small(e, k, False))))
        stage(i, LINE, final)
        for t in range(1, LINE + 1):
            stage(i, LINE + t, functools.partial(spread, t))
        stage(i, 2 * LINE, hand)
        stage(i, NS - 2, sent)
        stage(i, LAST - 1, finish)

    def wload(layer, j, x):
        return [near(nat[h].at[layer, :, at(j, FB)], wgu.at[x, :, pl.ds(FB * h, FB)], s_w.at[x, h]) for h in range(2)]

    def wdload(layer, j, x):
        return near(nat[DOWN].at[layer, at(j, FB)], wd.at[x], s_wd.at[x])

    def x_tile(t):
        return near(x.at[at(t, TT)], dgu.at[at(t, TT), pl.ds(0, D)], s_x.at[t])

    def h1_tile(t):
        return near(dgu.at[at(t, TT), pl.ds(0, D)], h1.at[at(t, TT)], s_h1.at[t])

    def dy_tile(t):
        return near(dy.at[at(t, TT)], dv.at[at(t, TT)], s_dy.at[t])

    def a0_load():
        return near(a0, av, s_a0)

    def a0_keep():
        return near(av, a0, s_a0)

    def keep(j):
        return near(dgu, dgu_all.at[j], s_dgu)

    def dl(u):
        return near(dgu_all.at[u % BLOCKS, at(u // BLOCKS, HALF)], dgu.at[at(u % 2, HALF)], s_dl.at[u % 2])

    def gl(s, put=False):
        e = s % 3
        here = [(t.at[at(s % TILES, TT), at(s // TILES, FB)], gt.at[e, h]) for h, t in enumerate((gate0, up0))]
        return [near(b, t, s_keep.at[e, h]) if put else near(t, b, s_gt.at[e, h]) for h, (t, b) in enumerate(here)]

    def h1_load():
        return near(h1, av, s_h)

    def g_out(layer, j, t):
        return [near(gout.at[t, :, :, :, pl.ds(FB * h, FB)], g[h].at[layer, t, :, :, :, at(j, FB)], s_go.at[t, h]) for h in range(2)]

    def _rms(b):
        wide = f(b)
        return (wide * lax.rsqrt(jnp.mean(wide * wide, -1, keepdims=True) + 1e-6)).astype(BF)

    def down(s):
        rows, j = at(s % TILES, TT), s // TILES
        acc[rows] = jnp.where(j == 0, 0.0, acc[rows]) + _dot(hid[at(s % 2, TT)], wd[j % 2], 1, 0)

    def close(t):
        rows = at(t, TT)
        new = (f(dgu[rows, :D]) + f(acc[rows].astype(BF))).astype(BF)
        dgu[rows, :D] = new
        av[rows] = _rms(new)
        h1_tile(t).start()

    STEPS = BLOCKS * TILES

    def forward(s):
        j, t = s // TILES, s % TILES
        k = j % 2
        rows = at(t, TT)

        @pl.when(t == 0)
        def _():
            wait(wload(0, j, k))
            wdload(0, j, k).wait()

        @pl.when(t == 1)
        def _():
            last = j == BLOCKS - 1
            layer, nxt = jnp.where(last, 1, 0), jnp.where(last, 0, j + 1)
            run(wload(layer, nxt, 1 - k))
            wdload(layer, nxt, 1 - k).start()

        pl.when(s == TILES)(lambda: a0_keep().start())
        pl.when(s == STEPS - TILES)(lambda: a0_keep().wait())
        pl.when(s >= 3)(lambda: wait(gl(s - 3, True)))

        @pl.when(j == 0)
        def _():
            x_tile(t).wait()
            av[rows] = _rms(dgu[rows, :D])

        gu = _dot(av[rows], wgu[k], 1, 0)
        down(jnp.where(s == 0, TILES - 1, s - 1))
        gate, up = gu[:, :FB], gu[:, FB:]
        gt[s % 3, 0] = gate
        gt[s % 3, 1] = up
        hid[at(s % 2, TT)] = (gate * jax.nn.sigmoid(gate) * up).astype(BF)
        run(gl(s, True))
        pl.when(s > STEPS - TILES)(lambda: close(t - 1))

    def gated(rows, gate, up, dh):
        s = jax.nn.sigmoid(gate)
        gs = gate * s
        dh = f(dh.astype(BF))
        hid[rows] = (gs * up).astype(BF)
        dgu[rows, FB:] = (dh * gs).astype(BF)
        dgu[rows, :FB] = (dh * up * (s + gs * (1 - s))).astype(BF)

    def gu_half(t, layer, j):
        out = _dot(av[:, at(t, TT)], dgu[...], 0, 0).astype(BF)
        gout[t] = out.reshape(gout.shape[1:])
        run(g_out(layer, j, t))

    def where(i):
        top, low = i < DA, (i >= LOW) & (i < END)
        ii = jnp.where(top, i, i - LOW)
        return top, low, ii // 4, ii % 4, jnp.where(top, 1, 0)

    def before(i):
        top, low, j, r, layer = where(i)

        @pl.when((top | low) & (r == 3))
        def _():
            for t in range(2):
                wait(g_out(layer, j, t))

        stage(i, LEAD, fetch)

    def compute(i):
        top, low, j, r, layer = where(i)
        x = jnp.where(top, j + 1, j) % 2

        pl.when(((i > 4) & (i <= DA + 1) & (i % 4 == 1)) | ((i > LOW + 4) & (i <= END + 1) & (i % 4 == (LOW + 1) % 4)))(lambda: near(dout, dout, s_do).wait())

        @pl.when(top & (r == 0))
        def _():
            wait(wload(1, j, x))
            wdload(1, j, x).wait()
            pl.when(j > 0)(lambda: keep(j - 1).wait())

            @pl.when(j < BLOCKS - 1)
            def _():
                run(wload(1, j + 1, 1 - x))
                wdload(1, j + 1, 1 - x).start()

        @pl.when(top & (r < 2))
        def _():
            def one(t):
                pl.when(j == 0)(lambda: wait((dy_tile(t), h1_tile(t))))
                rows = at(t, TT)
                gu = _dot(av[rows], wgu[x], 1, 0)
                gated(rows, gu[:, :FB], gu[:, FB:], _dot(dv[rows], wd[x], 1, 1))

            loop(2 * r, 2 * r + 2, one)
            pl.when(r == 1)(lambda: keep(j).start())

        @pl.when(low & (r == 0))
        def _():
            wdload(0, j, x).wait()
            pl.when(j < BLOCKS - 1)(lambda: wdload(0, j + 1, 1 - x).start())

        @pl.when(low & (r < 2))
        def _():
            def one(t):
                s = TILES * j + t
                wait(gl(s))
                pl.when(s < BLOCKS * TILES - 2)(lambda: run(gl(s + 2)))
                rows = at(t, TT)
                gated(rows, gt[s % 3, 0], gt[s % 3, 1], _dot(dv[rows], wd[x], 1, 1))

            loop(3 * r, 3 + r, one)

        @pl.when((top & (r == 2)) | (low & ((r == 1) | (r == 2))))
        def _():
            pl.when(i == LOW + 1)(lambda: a0_load().wait())
            loop(jnp.where(top, 0, r - 1), jnp.where(top, 2, r), lambda t: gu_half(t, layer, j))

        @pl.when((top | low) & (r == 3))
        def _():
            out = _dot(hid[...], dv[...], 0, 0)
            pp, n = dout.shape[:2]
            for p in range(pp):
                dout[p] = out[n * p : n * (p + 1)].astype(BF)

            def send(p):
                o = pp * j + p
                near(dout.at[p], g[DOWN].at[layer, o // 40, (o // 10) % LINE, (o // 5) % 2, o % 5], s_do).start()

            loop(0, pp, send)

        @pl.when(i == DA - 1)
        def _():
            keep(BLOCKS - 1).wait()
            run(wload(1, 0, 0))
            dl(0).start()
            h1_load().start()

        @pl.when((i >= DA) & (i < LOW))
        def _():
            u = i - DA
            j, x = u % BLOCKS, u % 2
            wait(wload(1, j, x))
            dl(u).wait()

            @pl.when(i < LOW - 1)
            def _():
                run(wload(1, (u + 1) % BLOCKS, 1 - x))
                dl(u + 1).start()

            half = u // BLOCKS
            sums = at(half, HALF)
            acc[sums] = jnp.where(j == 0, 0.0, acc[sums]) + _dot(dgu[at(x, HALF)], wgu[x], 1, 1)

            @pl.when(j == BLOCKS - 1)
            def _():
                pl.when(half == 0)(lambda: h1_load().wait())

                def one(t):
                    there = pl.ds(pl.multiple_of(half * HALF + t * 256, 256), 256)
                    wide, da = f(av[there]), acc[there]
                    scale = lax.rsqrt(jnp.mean(wide * wide, -1, keepdims=True) + 1e-6)
                    inner = jnp.mean(wide * da, -1, keepdims=True)
                    back = (scale * da - wide * (scale * scale * scale * inner)).astype(BF)
                    dv[there] = (f(dv[there]) + f(back)).astype(BF)

                loop(0, HALF // 256, one)
                pl.when(half == 1)(lambda: a0_load().start())

        @pl.when(i == LOW - 2)
        def _():
            wdload(0, 0, 0).start()
            run(gl(0))
            run(gl(1))

    x_tile(0).start()
    run(wload(0, 0, 0))
    wdload(0, 0, 0).start()
    run([x_tile(t) for t in range(1, TILES)] + [dy_tile(t) for t in range(TILES)])
    hid[...] = jnp.zeros_like(hid)
    loop(0, STEPS, forward)
    down(STEPS - 1)
    close(TILES - 1)
    for s in range(STEPS - 3, STEPS):
        wait(gl(s, True))
    pl.semaphore_wait(barrier, 2 + jnp.where(more, 1, 0) + jnp.where(less, 1, 0))

    def tick(i):
        before(i)
        compute(i)
        communicate(i - LEAD)

    loop(0, N + LAST + LEAD, tick)


def step_scratch():
    d = pltpu.SemaphoreType.DMA
    ry, rz = ROWS

    def vm(*shape, dtype=BF):
        return pltpu.VMEM(shape, dtype)

    sums = [vm(NS, 2, LINE, r, LANES) for _ in range(2) for r in (ry, rz)]
    lines = [vm(NS, LINE, *r, LANES) for _ in range(2) for r in ((ry,), (2, rz))]
    small = [vm(n, *SHAPE[i], dtype=t) for n, t in ((NL, F32), (NL, F32), (NW, BF)) for i in (UP, DOWN)]
    ring, two, four, three = d((NS,)), d((NS, 2)), d((2, NS, LINE)), d((NS, LINE - 1))
    sems = [two, two, two, ring, ring, four, four, four, four, ring, ring, d((NL, 3)), d((NL, 3))]
    sems += [three] * 4 + [d((NS, 2 * LINE - 1))] * 2 + [three] * 4 + [ring, ring, ring, d((2 * NS,))]
    work = [vm(T, D), vm(T, D), vm(2, D, 2 * FB), vm(2, FB, D), vm(T, FB), vm(T, 2 * FB), vm(2, LINE, 2, D // 16, 2 * FB), vm(16, 40, D)]
    work += [vm(T, D, dtype=F32), vm(3, 2, TT, FB, dtype=F32)]
    work += [d((TILES,)), d((TILES,)), d((2, 2)), d((2,)), d, d((2, 2)), d, d((2,)), d((3, 2)), d, d, d((3, 2)), d((TILES,))]
    return [*sums, *lines, *small, vm(NS, LINE, ry, LANES), vm(NS, rz, LANES), *sems, *work]


def hbm(n):
    return [pl.BlockSpec(memory_space=pl.ANY)] * n


def step_of(x, dy, w, m, v):
    def blocks(t, *tail):
        return (t.shape[0], 2, LINE, 2, *(tail or (t.shape[1] // 16,)), t.shape[-1])

    like = jax.ShapeDtypeStruct
    views = [t.reshape(blocks(t)) for t in w]
    args = [x, dy, *w, *views, *m, *v]
    outs = [like(t.shape, BF) for t in views] + [like(t.shape, F32) for t in (*m, *v)]
    outs += [like(t.shape, BF) for t in views[:DOWN]] + [like(blocks(w[DOWN], 5, 40), BF), like((BLOCKS, T, 2 * FB), BF)]
    outs += [like((T, F), F32)] * 2 + [like((T, D), BF)] * 2
    new = pl.pallas_call(
        step_kernel,
        out_shape=outs,
        in_specs=hbm(len(args)),
        out_specs=hbm(len(outs)),
        scratch_shapes=step_scratch(),
        compiler_params=pltpu.CompilerParams(collective_id=0, has_side_effects=True, vmem_limit_bytes=67043328),
    )(*args)
    old = (*w, *m, *v)
    return copied([n.reshape(t.shape) for n, t in zip(new, old)])


def copy_kernel(n, *refs):
    src, dst, tmp = refs[:n], refs[n : 2 * n], refs[2 * n : 3 * n]
    s_in, s_out = refs[3 * n :]
    cuts = [(k, l, at(b, t.shape[1] // 4)) for k, t in enumerate(src) for l in range(2) for b in range(4 if t.dtype == BF else 0)]
    cuts += [(k, l, ALL) for k, t in enumerate(src) for l in range(2) if t.dtype == F32]
    ins = [near(src[k].at[l, r], tmp[k].at[l, r], s_in.at[e]) for e, (k, l, r) in enumerate(cuts)]
    outs = [near(tmp[k].at[l, r], dst[k].at[l, r], s_out.at[e]) for e, (k, l, r) in enumerate(cuts)]
    run(ins)
    for i, o in zip(ins, outs, strict=True):
        i.wait()
        o.start()
    wait(outs)


def copied(arrays):
    n = len(arrays)
    many = sum(8 if t.dtype == BF else 2 for t in arrays)
    return pl.pallas_call(
        functools.partial(copy_kernel, n),
        out_shape=[jax.ShapeDtypeStruct(t.shape, t.dtype) for t in arrays],
        in_specs=hbm(n),
        out_specs=hbm(n),
        scratch_shapes=[pltpu.VMEM(t.shape, t.dtype) for t in arrays] + [pltpu.SemaphoreType.DMA((many,))] * 2,
        compiler_params=pltpu.CompilerParams(vmem_limit_bytes=67043328),
    )(*arrays)


def solution(mesh):
    def step(x, dy, *arrays):
        w, m, v = (arrays[i : i + 3] for i in (0, 3, 6))
        return tuple(step_of(x[0], dy[0], w, m, v))

    one, whole, rows = P(("rep", "dp")), P(), P(None, "dp")
    return jax.shard_map(
        step,
        mesh=mesh,
        in_specs=(one, one) + (whole,) * 3 + (rows,) * 6,
        out_specs=(P("rep"),) * 3 + (P("rep", "dp"),) * 6,
        check_vma=False,
    )
```

time: 1760 us -> 479 us (0.27)
  waiting for transfers between devices: 707 us -> 0 us
  Pallas kernels: 0 us -> 478 us
  matrix products: 461 us -> 0 us
  starting transfers between devices: 299 us -> 0 us
  other arithmetic: 119 us -> 0 us
  local copies, waits for them, and re-layouts: 106 us -> 0 us
  loops' own time: 49.7 us -> 0 us
    dot_general x102 -> x0, waiting for transfers between devices: 604 us -> none  [the longest x34 220 us: layer(): up = jnp.dot(a, w['w_up'], preferred_element_type=jnp.float32)]
    pallas_call x0 -> x2, Pallas kernels: none -> 478 us  [the longest x1 444 us: step_of(): pl.pallas_call(step_kernel, out_shape=outs, in_specs=hbm(len(args)), out_...]
    dot_general x57 -> x0, matrix products: 461 us -> none  [the longest x19 171 us: matmul(): jnp.dot(a, w, preferred_element_type=jnp.float32).astype(jnp.bfloat16)]
    dot_general x102 -> x0, starting transfers between devices: 299 us -> none  [the longest x34 134 us: layer(): up = jnp.dot(a, w['w_up'], preferred_element_type=jnp.float32)]
    reshape x3 -> x0, waiting for transfers between devices: 103 us -> none  [step(): t.reshape(-1, *t.shape[2:])]
    unnamed x57 -> x0, local copies, waits for them, and re-layouts: 89.9 us -> none
    dot_general x112 -> x0, other arithmetic: 82.8 us -> none
    another operation x6 -> x0, loops' own time: 49.7 us -> none  [the longest x2 17.2 us: layer(): up = jnp.dot(a, w['w_up'], preferred_element_type=jnp.float32)]
  transfers between devices with their start and end apart: 105 -> 0, of which waited for: 63 -> 0; matrix products, arithmetic and copies ran while one was open for 21% -> 0% of each run, Pallas kernels for 0% -> 0%
where the time goes in v2:
time: 479 us
  Pallas kernels  478 us (100%)
    pallas_call x1, Pallas kernels, step_of(): pl.pallas_call(step_kernel, out_shape=outs, in_specs=hbm(len(args)), out_...  444 us
    pallas_call x1, Pallas kernels, copied(): pl.pallas_call(functools.partial(copy_kernel, n), out_shape=[jax.ShapeDty...  33.3 us

profile of v2, /device:TPU:0, one launch (start us, length us, event | category | flops | bytes accessed | tf_op | source)
XLA Modules:
  0.0 478.5 jit_solution(18326108593003212617)
XLA Ops:
  0.6 444.4 %shard_map.178 = (bf16[2,2,4,2,64,3200]{5,4,3,2,1,0:T(8,128)(2,1)}, bf16[2,2,4,2,64,3200]{5,4,3,2,1,0:T(8,128)(2,1)}, bf16[2,2,4,2,200,1024]{5,4,3,2,1,0:T(8,128...) custom-call(bf16[2048,1024]{1,0:T(8,128)(2,1)} %bitcast.14, ...), custom_call_target="tpu_custom_call" | custom-call | tf_op jit(solution)/shard_map/pallas_call | solution.py:638
  445.1 33.3 %shard_map.179 = (bf16[2,1024,3200]{2,1,0:T(8,128)(2,1)}, bf16[2,1024,3200]{2,1,0:T(8,128)(2,1)}, bf16[2,3200,1024]{2,1,0:T(8,128)(2,1)}, f32[2,64,3200]{2,1,0:T...) custom-call(bf16[2,1024,3200]{2,1,0:T(8,128)(2,1)} %bitcast.11, ...), custom_call_target="tpu_custom_call" | custom-call | tf_op jit(solution)/shard_map/pallas_call | solution.py:667

commit v3 on v2

--- a/solution.py
+++ b/solution.py
@@ -92,11 +92,11 @@
         return out
 
     x, dy = take(2)
-    nat, w, m, v, ow, om, ov, g = (take(3) for _ in range(8))
+    nat, w, m, v, ow, om, ov = (take(3) for _ in range(7))
+    g_gu, g_down = take(2)
     dgu_all, gate0, up0, a0, h1 = take(5)
     own, oth, rr, ll, mbuf, vbuf, wbuf = (take(2) for _ in range(7))
-    (ry, ryz, s_own, s_e, r_e, s_y, r_y, s_zr, r_zr, s_zl, r_zl, s_yz, r_yz, s_ld, s_st,
-     s_ar, r_ar, s_al, r_al, s_ay, r_ay, s_br, r_br, s_bl, r_bl, s_by, r_by, s_c, r_c,
+    (ry, ryz, s_own, s_e, r_e, s_y, r_y, s_zr, r_zr, s_zl, r_zl, s_yz, r_yz, s_ld, s_st, s_ag, r_ag, s_c, r_c,
      av, dv, wgu, wd, hid, dgu, gout, dout, acc, gt,
      s_x, s_dy, s_w, s_wd, s_dgu, s_go, s_do, s_dl, s_gt, s_h, s_a0, s_keep, s_h1) = refs
     rep, dp = lax.axis_index("rep"), lax.axis_index("dp")
@@ -134,6 +134,13 @@
         for i in SHAPE:
             pl.when(kind == i)(functools.partial(one, i))
 
+    def chip(do):
+        def one(zz):
+            do(zz)
+
+        for zz in range(LINE):
+            pl.when(z == zz)(functools.partial(one, zz))
+
     def stage(tick, st, do):
         k = tick - st
         pl.when((k >= 0) & (k < N))(lambda: do(k, k % NS))
@@ -141,18 +148,21 @@
     def fetch(k, q):
         layer, kind, s = what(k)
 
-        def of(i):
-            rows, cols = cut(i, s)
-            for part, d0, n, s0, col in pieces(i):
-                cc = pl.ds(cols.start + col * LANES, LANES)
-                here = (pl.ds(rows.start + s0, n), cc) if i < DOWN else (s // MANY, pl.ds(s0, n), cc)
-                to = (q, ALL, ALL, pl.ds(d0, n))
-                mine, other = ((layer, ALL, ALL, h, *here) for h in (c, 1 - c))
-                src = g[i]
-                near(src.at[mine], own[part].at[to], s_own.at[q, part]).start()
-                far(src.at[other], oth[part].at[to], s_e.at[q, part], r_e.at[q, part], core).start()
-
-        each(kind, of)
+        def both(src, dst, part):
+            near(src(c), own[part].at[dst], s_own.at[q, part]).start()
+            far(src(1 - c), oth[part].at[dst], s_e.at[q, part], r_e.at[q, part], core).start()
+
+        @pl.when(kind < DOWN)
+        def _():
+            for part, d0 in enumerate((0, ROWS[0])):
+                both(lambda h: g_gu.at[layer, s // MANY, :, kind, s % MANY, :, h, pl.ds(d0, ROWS[part])], q, part)
+
+        @pl.when(kind == DOWN)
+        def _():
+            cols = cut(DOWN, s)[1].start
+            for part, d0, n, s0, col in pieces(DOWN):
+                here = (s // MANY, pl.ds(s0, n), pl.ds(cols + col * LANES, LANES))
+                both(lambda h: g_down.at[(layer, ALL, ALL, h, *here)], (q, ALL, ALL, pl.ds(d0, n)), part)
 
     def exchange(q, part):
         return far(own[part].at[q], oth[part].at[q], s_e.at[q, part], r_e.at[q, part], core)
@@ -171,39 +181,44 @@
         loop(0, LINE, add)
         y_send(q).start()
 
-    def line(part, q, d, to_right):
+    def span(zz, to_right):
+        return (zz + 1, LINE) if to_right else (0, zz)
+
+    def line(part, q, zz, to_right):
         ss, rs, buf, to = (s_zr, r_zr, rr, right) if to_right else (s_zl, r_zl, ll, left)
-        src = own[0].at[q, y, d] if part == 0 else own[1].at[q, :, d]
-        return far(src, buf[part].at[q, d], ss.at[part, q, d], rs.at[part, q, d], to)
+        lo, hi = span(zz, to_right)
+        d = pl.ds(lo, hi - lo)
+        src, dst = (own[0].at[q, y, d], buf[0].at[q, d]) if part == 0 else (own[1].at[q, :, d], buf[1].at[q, :, d])
+        return far(src, dst, ss.at[part, q], rs.at[part, q], to)
 
     def total(part, q, d, buf):
         if part == 0:
             own[0][q, y, d] = (f(own[0][q, y, d]) + f(oth[0][q, y, d]) + f(ry[q, d]) + f(buf[0][q, d])).astype(BF)
         else:
             for j in range(2):
-                own[1][q, j, d] = (f(own[1][q, j, d]) + f(oth[1][q, j, d]) + f(buf[1][q, d, j])).astype(BF)
-
-    def go(to_right, part, k, q):
-        def get(d):
-            line(part, q, d, to_right).wait_recv()
-
-        def give(d):
+                own[1][q, j, d] = (f(own[1][q, j, d]) + f(oth[1][q, j, d]) + f(buf[1][q, j, d])).astype(BF)
+
+    def go(to_right, part, zz, k, q):
+        back = zz - 1 if to_right else zz + 1
+        if 0 <= back < LINE:
+            line(part, q, back, to_right).wait_recv()
+        lo, hi = span(zz, to_right)
+        for d in range(lo, hi):
             total(part, q, d, rr if to_right else ll)
-            line(part, q, d, to_right).start()
-
-        if to_right:
-            pl.when(less)(lambda: loop(z, LINE, get))
-            loop(z + 1, LINE, give)
-        else:
-            pl.when(more)(lambda: loop(0, z + 1, get))
-            loop(0, z, give)
+        if lo < hi:
+            line(part, q, zz, to_right).start()
+
+    def lines(i, zz):
+        for part in (1, 0):
+            for to_right, steps in ((True, zz), (False, LINE - 1 - zz)):
+                stage(i, 1 - part + steps, functools.partial(go, to_right, part, zz))
 
     def yz_send(q):
         return far(own[1].at[q, 1 - y, z], ryz.at[q], s_yz.at[q], r_yz.at[q], across)
 
     def yz(k, q):
-        b, r = (q, 1 - y, z), (q, z, 1 - y)
-        own[1][b] = (f(own[1][b]) + f(oth[1][b]) + f(rr[1][r]) + f(ll[1][r])).astype(BF)
+        b = (q, 1 - y, z)
+        own[1][b] = (f(own[1][b]) + f(oth[1][b]) + f(rr[1][b]) + f(ll[1][b])).astype(BF)
         yz_send(q).start()
 
     def small(i, k, put):
@@ -225,7 +240,7 @@
             for part, d0, n, s0, col in pieces(i):
                 r = pl.ds(d0, n)
                 gr = f(own[part][q, y, z, r]) + f(oth[part][q, y, z, r])
-                gr += f(ry[q, z, r]) + f(rr[0][q, z, r]) + f(ll[0][q, z, r]) if part == 0 else f(rr[1][q, z, y, r]) + f(ll[1][q, z, y, r]) + f(ryz[q, r])
+                gr += f(ry[q, z, r]) + f(rr[0][q, z, r]) + f(ll[0][q, z, r]) if part == 0 else f(rr[1][q, y, z, r]) + f(ll[1][q, y, z, r]) + f(ryz[q, r])
                 gr = f(gr.astype(BF))
                 b = (pl.ds(s0, n), pl.ds(col * LANES, LANES))
                 bm, bw = (k % NL, *b), (k % NW, *b)
@@ -238,78 +253,43 @@
             run(small(i, k, True))
 
         each(what(k)[1], of)
-        spread(0, k, q)
-
-    def moves(i, k, q, t):
+
+    def move(e, i, k, q, zz):
         layer, _, s = what(k)
-        dst = ow[i]
-
-        def block(part, by, bz):
-            return dst.at[(layer, by, bz, c, *cut(i, s, part))]
-
-        def mine(part):
-            r, cc = SHAPE[i][0] if i < DOWN else FIRST[i][0], FIRST[i][1]
-            if part:
-                r, cc = (pl.ds(0, r), pl.ds(cc, FB - cc)) if i < DOWN else (pl.ds(r, SHAPE[i][0] - r), pl.ds(0, cc))
-            else:
-                r, cc = pl.ds(0, r), pl.ds(0, cc)
-            return wbuf[i // DOWN].at[k % NW, r, cc]
-
-        def same(ref, ss, rs, n, to, src=None):
-            n = q if n is None else (q, n)
-            return lambda: far(ref if src is None else src, ref, ss.at[n], rs.at[n], to)
-
-        def along(part, b, n, src=None):
-            sr, gr, sl, gl_ = (s_ar, r_ar, s_al, r_al) if part == 0 else (s_br, r_br, s_bl, r_bl)
-            return same(b, sr, gr, n, right, src), same(b, sl, gl_, n, left, src)
-
-        out = []
+        part = e // 3
+        along = e % 4
+        lo, hi = (0, zz + 1) if e in (0, 4) else (zz, LINE) if e in (1, 5) else (0, LINE) if part == 0 else (zz, zz + 1)
+        blocks = lo if hi - lo == 1 else pl.ds(lo, hi - lo)
+        dst = ow[i].at[(layer, ALL if e > 3 else y, blocks, c, *cut(i, s, part))]
+        src = dst
+        if hi - lo == 1 and e < 4:
+            (r, cc), (r0, c0) = SHAPE[i], FIRST[i]
+            rows = (pl.ds(r0, r - r0) if part else pl.ds(0, r0)) if i == DOWN else pl.ds(0, r)
+            cols = pl.ds(0, cc) if i == DOWN else pl.ds(c0, cc - c0) if part else pl.ds(0, c0)
+            src = wbuf[i // DOWN].at[k % NW, rows, cols]
+        to = (right, left)[along] if along < 2 else across
+        return far(src, dst, s_ag.at[e, q], r_ag.at[e, q], to)
+
+    def events(zz):
         side = LINE - 1
-        b, e = block(0, y, z), block(1, y, z)
-        if t == 0:
-            r, l = along(0, b, 0, mine(0))
-            out.append((None, None, [(more, r), (less, l), (None, same(b, s_ay, r_ay, 0, across, mine(0))), (None, same(e, s_by, r_by, None, across, mine(1)))]))
-        elif t <= side:
-            for sign, on in ((-1, z >= t), (1, z + t <= side)):
-                b = block(0, y, z + sign * t)
-                to = 0 if sign < 0 else 1
-                sends = [(None, same(b, s_ay, r_ay, t if sign < 0 else side + t, across))]
-                if t < side:
-                    sends.insert(0, ((more, less)[to], along(0, b, t)[to]))
-                out.append((on, along(0, b, t - 1)[to], sends))
-        u = t - 1
-        if u >= 0:
-            for sign, on in ((-1, z >= u), (1, z + u <= side))[: 1 if u == 0 else 2]:
-                b = block(0, 1 - y, z + sign * u)
-                out.append((on, same(b, s_ay, r_ay, u if sign < 0 else side + u, across), []))
-        if u == 0:
-            r, l = along(1, dst.at[(layer, ALL, z, c, *cut(i, s, 1))], 0)
-            out.append((None, same(e, s_by, r_by, None, across), [(more, r), (less, l)]))
-        elif u > 0:
-            for sign, on in ((-1, z >= u), (1, z + u <= side)):
-                b = dst.at[(layer, ALL, z + sign * u, c, *cut(i, s, 1))]
-                to = 0 if sign < 0 else 1
-                out.append((on, along(1, b, u - 1)[to], [((more, less)[to], along(1, b, u)[to])] if u < side else []))
+        turn = max(zz, side - zz)
+        out = [(0, None, 3), (1, (3, zz), None), (turn, None, 2), (turn + 1, (2, zz), None)]
+        for part in range(2):
+            for t, back, e, more_ in ((zz, zz - 1, 0, zz < side), (side - zz, zz + 1, 1, zz > 0)):
+                e += 4 * part
+                out.insert(0, (t + part, (e, back) if 0 <= back < LINE else None, e if more_ else None))
         return out
 
-    def when(cond, do):
-        do() if cond is None else pl.when(cond)(lambda: do())
-
-    def spread(t, k, q):
-        def of(i):
-            if t == 1:
-                wait(small(i, k, True))
-            for cond, first_, sends in moves(i, k, q, t):
-
-                def act(first_=first_, sends=sends):
-                    if first_ is not None:
-                        first_().wait_recv()
-                    for on, copy in sends:
-                        when(on, lambda copy=copy: copy().start())
-
-                when(cond, act)
-
-        each(what(k)[1], of)
+    def spread(t, zz, k, q):
+        todo = [(w_, e) for step, w_, e in events(zz) if step == t]
+        if t == 1:
+            wait(small(GATE, k, True))
+        for w_, _ in todo:
+            if w_:
+                move(w_[0], GATE, k, q, w_[1]).wait_recv()
+        sends = [e for _, e in todo if e is not None]
+        if sends:
+            each(what(k)[1], lambda i: run([move(e, i, k, q, zz) for e in sends]))
 
     def over(i, k, q):
         layer, _, s = what(k)
@@ -319,44 +299,37 @@
     def hand(k, q):
         each(what(k)[1], lambda i: over(i, k, q).start())
 
-    def finish(k, q):
-        def of(i):
-            over(i, k, q).wait()
-            for t in range(LINE + 1):
-                for cond, _, sends in moves(i, k, q, t):
-
-                    def act(sends=sends):
-                        for on, copy in sends:
-                            when(on, lambda copy=copy: copy().wait_send())
-
-                    if sends:
-                        when(cond, act)
-
-        each(what(k)[1], of)
-
-    def sent(k, q):
+    def finish(zz, k, q):
+        over(GATE, k, q).wait()
+        for _, _, e in events(zz):
+            if e is not None:
+                move(e, GATE, k, q, zz).wait_send()
+
+    def sent(zz, k, q):
         for part in range(2):
             exchange(q, part).wait_send()
-            loop(z + 1, LINE, lambda d, part=part: line(part, q, d, True).wait_send())
-            loop(0, z, lambda d, part=part: line(part, q, d, False).wait_send())
+            for to_right in (True, False):
+                lo, hi = span(zz, to_right)
+                if lo < hi:
+                    line(part, q, zz, to_right).wait_send()
         y_send(q).wait_send()
         yz_send(q).wait_send()
+
+    def spreads(i, zz):
+        for t in range(LINE + 1):
+            stage(i, LINE + t, functools.partial(spread, t, zz))
+        stage(i, NS - 2, functools.partial(sent, zz))
+        stage(i, LAST - 1, functools.partial(finish, zz))
 
     def communicate(i):
         stage(i, 0, first)
         stage(i, 1, lambda k, q: y_send(q).wait_recv())
-        for part in (1, 0):
-            base = 1 - part
-            stage(i, base + z, functools.partial(go, True, part))
-            stage(i, base + LINE - 1 - z, functools.partial(go, False, part))
+        chip(lambda zz: lines(i, zz))
         stage(i, LINE - 1, yz)
         stage(i, LINE - 2, lambda k, q: each(what(k)[1], lambda e: run(small(e, k, False))))
         stage(i, LINE, final)
-        for t in range(1, LINE + 1):
-            stage(i, LINE + t, functools.partial(spread, t))
+        chip(lambda zz: spreads(i, zz))
         stage(i, 2 * LINE, hand)
-        stage(i, NS - 2, sent)
-        stage(i, LAST - 1, finish)
 
     def wload(layer, j, x):
         return [near(nat[h].at[layer, :, at(j, FB)], wgu.at[x, :, pl.ds(FB * h, FB)], s_w.at[x, h]) for h in range(2)]
@@ -394,7 +367,7 @@
         return near(h1, av, s_h)
 
     def g_out(layer, j, t):
-        return [near(gout.at[t, :, :, :, pl.ds(FB * h, FB)], g[h].at[layer, t, :, :, :, at(j, FB)], s_go.at[t, h]) for h in range(2)]
+        return near(gout.at[t], g_gu.at[layer, j, t], s_go.at[t])
 
     def _rms(b):
         wide = f(b)
@@ -413,7 +386,7 @@
 
     STEPS = BLOCKS * TILES
 
-    def forward(s):
+    def forward(closing, s):
         j, t = s // TILES, s % TILES
         k = j % 2
         rows = at(t, TT)
@@ -433,20 +406,15 @@
         pl.when(s == TILES)(lambda: a0_keep().start())
         pl.when(s == STEPS - TILES)(lambda: a0_keep().wait())
         pl.when(s >= 3)(lambda: wait(gl(s - 3, True)))
-
-        @pl.when(j == 0)
-        def _():
-            x_tile(t).wait()
-            av[rows] = _rms(dgu[rows, :D])
-
         gu = _dot(av[rows], wgu[k], 1, 0)
         down(jnp.where(s == 0, TILES - 1, s - 1))
         gate, up = gu[:, :FB], gu[:, FB:]
         gt[s % 3, 0] = gate
         gt[s % 3, 1] = up
         hid[at(s % 2, TT)] = (gate * jax.nn.sigmoid(gate) * up).astype(BF)
+        if closing:
+            close(t - 1)
         run(gl(s, True))
-        pl.when(s > STEPS - TILES)(lambda: close(t - 1))
 
     def gated(rows, gate, up, dh):
         s = jax.nn.sigmoid(gate)
@@ -458,8 +426,13 @@
 
     def gu_half(t, layer, j):
         out = _dot(av[:, at(t, TT)], dgu[...], 0, 0).astype(BF)
-        gout[t] = out.reshape(gout.shape[1:])
-        run(g_out(layer, j, t))
+        many = FB // LANES
+        r = SHAPE[GATE][0]
+        for n in range(2 * many):
+            part = out[:, LANES * n : LANES * (n + 1)].reshape(LINE, 2, MANY, r, LANES)
+            for b in range(MANY):
+                gout[t, n // many, b, :, :, pl.ds(n % many * r, r)] = part[:, :, b]
+        g_out(layer, j, t).start()
 
     def where(i):
         top, low = i < DA, (i >= LOW) & (i < END)
@@ -471,8 +444,7 @@
 
         @pl.when((top | low) & (r == 3))
         def _():
-            for t in range(2):
-                wait(g_out(layer, j, t))
+            wait([g_out(layer, j, t) for t in range(2)])
 
         stage(i, LEAD, fetch)
 
@@ -495,8 +467,12 @@
 
         @pl.when(top & (r < 2))
         def _():
+            @pl.when(j == 0)
+            def _():
+                for t in range(2):
+                    wait((dy_tile(2 * r + t), h1_tile(2 * r + t)))
+
             def one(t):
-                pl.when(j == 0)(lambda: wait((dy_tile(t), h1_tile(t))))
                 rows = at(t, TT)
                 gu = _dot(av[rows], wgu[x], 1, 0)
                 gated(rows, gu[:, :FB], gu[:, FB:], _dot(dv[rows], wd[x], 1, 1))
@@ -534,7 +510,7 @@
 
             def send(p):
                 o = pp * j + p
-                near(dout.at[p], g[DOWN].at[layer, o // 40, (o // 10) % LINE, (o // 5) % 2, o % 5], s_do).start()
+                near(dout.at[p], g_down.at[layer, o // 40, (o // 10) % LINE, (o // 5) % 2, o % 5], s_do).start()
 
             loop(0, pp, send)
 
@@ -587,7 +563,14 @@
     wdload(0, 0, 0).start()
     run([x_tile(t) for t in range(1, TILES)] + [dy_tile(t) for t in range(TILES)])
     hid[...] = jnp.zeros_like(hid)
-    loop(0, STEPS, forward)
+
+    def norm(t):
+        x_tile(t).wait()
+        av[at(t, TT)] = _rms(dgu[at(t, TT), :D])
+
+    loop(0, TILES, norm)
+    loop(0, STEPS - TILES + 1, functools.partial(forward, False))
+    loop(STEPS - TILES + 1, STEPS, functools.partial(forward, True))
     down(STEPS - 1)
     close(TILES - 1)
     for s in range(STEPS - 3, STEPS):
@@ -610,14 +593,13 @@
         return pltpu.VMEM(shape, dtype)
 
     sums = [vm(NS, 2, LINE, r, LANES) for _ in range(2) for r in (ry, rz)]
-    lines = [vm(NS, LINE, *r, LANES) for _ in range(2) for r in ((ry,), (2, rz))]
+    lines = [vm(NS, *r, LANES) for _ in range(2) for r in ((LINE, ry), (2, LINE, rz))]
     small = [vm(n, *SHAPE[i], dtype=t) for n, t in ((NL, F32), (NL, F32), (NW, BF)) for i in (UP, DOWN)]
-    ring, two, four, three = d((NS,)), d((NS, 2)), d((2, NS, LINE)), d((NS, LINE - 1))
-    sems = [two, two, two, ring, ring, four, four, four, four, ring, ring, d((NL, 3)), d((NL, 3))]
-    sems += [three] * 4 + [d((NS, 2 * LINE - 1))] * 2 + [three] * 4 + [ring, ring, ring, d((2 * NS,))]
-    work = [vm(T, D), vm(T, D), vm(2, D, 2 * FB), vm(2, FB, D), vm(T, FB), vm(T, 2 * FB), vm(2, LINE, 2, D // 16, 2 * FB), vm(16, 40, D)]
+    ring, two, parts, six = d((NS,)), d((NS, 2)), d((2, NS)), d((6, NS))
+    sems = [two, two, two, ring, ring, parts, parts, parts, parts, ring, ring, d((NL, 3)), d((NL, 3)), six, six, ring, d((2 * NS,))]
+    work = [vm(T, D), vm(T, D), vm(2, D, 2 * FB), vm(2, FB, D), vm(T, FB), vm(T, 2 * FB), vm(2, 2, MANY, LINE, 2, ry + rz, LANES), vm(16, 40, D)]
     work += [vm(T, D, dtype=F32), vm(3, 2, TT, FB, dtype=F32)]
-    work += [d((TILES,)), d((TILES,)), d((2, 2)), d((2,)), d, d((2, 2)), d, d((2,)), d((3, 2)), d, d, d((3, 2)), d((TILES,))]
+    work += [d((TILES,)), d((TILES,)), d((2, 2)), d((2,)), d, d((2,)), d, d((2,)), d((3, 2)), d, d, d((3, 2)), d((TILES,))]
     return [*sums, *lines, *small, vm(NS, LINE, ry, LANES), vm(NS, rz, LANES), *sems, *work]
 
 
@@ -633,7 +615,7 @@
     views = [t.reshape(blocks(t)) for t in w]
     args = [x, dy, *w, *views, *m, *v]
     outs = [like(t.shape, BF) for t in views] + [like(t.shape, F32) for t in (*m, *v)]
-    outs += [like(t.shape, BF) for t in views[:DOWN]] + [like(blocks(w[DOWN], 5, 40), BF), like((BLOCKS, T, 2 * FB), BF)]
+    outs += [like((2, BLOCKS, 2, 2, MANY, LINE, 2, sum(ROWS), LANES), BF), like(blocks(w[DOWN], 5, 40), BF), like((BLOCKS, T, 2 * FB), BF)]
     outs += [like((T, F), F32)] * 2 + [like((T, D), BF)] * 2
     new = pl.pallas_call(
         step_kernel,

time: 479 us -> 469 us (0.979)
  Pallas kernels: 478 us -> 467 us
    pallas_call x1, Pallas kernels: 444 us -> 434 us  [step_of(): pl.pallas_call(step_kernel, out_shape=outs, in_specs=hbm(len(args)), out_...]
where the time goes in v3:
time: 469 us; the launch traced here: 468 us
  Pallas kernels  467 us (100%)
    pallas_call x1, Pallas kernels, step_of(): pl.pallas_call(step_kernel, out_shape=outs, in_specs=hbm(len(args)), out_...  434 us
    pallas_call x1, Pallas kernels, copied(): pl.pallas_call(functools.partial(copy_kernel, n), out_shape=[jax.ShapeDty...  33.3 us

profile of v3, /device:TPU:0, one launch (start us, length us, event | category | flops | bytes accessed | tf_op | source)
XLA Modules:
  0.0 468.3 jit_solution(17530356019725877562)
XLA Ops:
  0.6 434.2 %shard_map.178 = (bf16[2,2,4,2,64,3200]{5,4,3,2,1,0:T(8,128)(2,1)}, bf16[2,2,4,2,64,3200]{5,4,3,2,1,0:T(8,128)(2,1)}, bf16[2,2,4,2,200,1024]{5,4,3,2,1,0:T(8,128...) custom-call(bf16[2048,1024]{1,0:T(8,128)(2,1)} %bitcast.14, ...), custom_call_target="tpu_custom_call" | custom-call | tf_op jit(solution)/shard_map/pallas_call | solution.py:620
  434.8 33.3 %shard_map.179 = (bf16[2,1024,3200]{2,1,0:T(8,128)(2,1)}, bf16[2,1024,3200]{2,1,0:T(8,128)(2,1)}, bf16[2,3200,1024]{2,1,0:T(8,128)(2,1)}, f32[2,64,3200]{2,1,0:T...) custom-call(bf16[2,1024,3200]{2,1,0:T(8,128)(2,1)} %bitcast.11, ...), custom_call_target="tpu_custom_call" | custom-call | tf_op jit(solution)/shard_map/pallas_call | solution.py:649

commit v4 on v3

--- a/solution.py
+++ b/solution.py
@@ -386,35 +386,37 @@
 
     STEPS = BLOCKS * TILES
 
-    def forward(closing, s):
-        j, t = s // TILES, s % TILES
-        k = j % 2
-        rows = at(t, TT)
-
-        @pl.when(t == 0)
+    def forward(p, closing=()):
+        j = p // 2
+        k, s = j % 2, 2 * p
+
+        @pl.when(p % 2 == 0)
         def _():
             wait(wload(0, j, k))
             wdload(0, j, k).wait()
 
-        @pl.when(t == 1)
+        @pl.when(p % 2 == 1)
         def _():
             last = j == BLOCKS - 1
             layer, nxt = jnp.where(last, 1, 0), jnp.where(last, 0, j + 1)
             run(wload(layer, nxt, 1 - k))
             wdload(layer, nxt, 1 - k).start()
 
-        pl.when(s == TILES)(lambda: a0_keep().start())
+        pl.when(p == 2)(lambda: a0_keep().start())
         pl.when(s == STEPS - TILES)(lambda: a0_keep().wait())
-        pl.when(s >= 3)(lambda: wait(gl(s - 3, True)))
-        gu = _dot(av[rows], wgu[k], 1, 0)
-        down(jnp.where(s == 0, TILES - 1, s - 1))
-        gate, up = gu[:, :FB], gu[:, FB:]
-        gt[s % 3, 0] = gate
-        gt[s % 3, 1] = up
-        hid[at(s % 2, TT)] = (gate * jax.nn.sigmoid(gate) * up).astype(BF)
-        if closing:
-            close(t - 1)
-        run(gl(s, True))
+        pl.when(p > 1)(lambda: wait(gl(s - 3, True)))
+        pl.when(p > 0)(lambda: wait(gl(s - 2, True)))
+        for e in range(2):
+            n = s + e
+            gu = _dot(av[at(n % TILES, TT)], wgu[k], 1, 0)
+            down(jnp.where(n == 0, TILES - 1, n - 1))
+            gate, up = gu[:, :FB], gu[:, FB:]
+            gt[n % 3, 0] = gate
+            gt[n % 3, 1] = up
+            hid[at(n % 2, TT)] = (gate * jax.nn.sigmoid(gate) * up).astype(BF)
+            if e in closing:
+                close((n - 1) % TILES)
+            run(gl(n, True))
 
     def gated(rows, gate, up, dh):
         s = jax.nn.sigmoid(gate)
@@ -477,7 +479,8 @@
                 gu = _dot(av[rows], wgu[x], 1, 0)
                 gated(rows, gu[:, :FB], gu[:, FB:], _dot(dv[rows], wd[x], 1, 1))
 
-            loop(2 * r, 2 * r + 2, one)
+            one(2 * r)
+            one(2 * r + 1)
             pl.when(r == 1)(lambda: keep(j).start())
 
         @pl.when(low & (r == 0))
@@ -496,10 +499,15 @@
 
             loop(3 * r, 3 + r, one)
 
-        @pl.when((top & (r == 2)) | (low & ((r == 1) | (r == 2))))
+        @pl.when(top & (r == 2))
+        def _():
+            gu_half(0, layer, j)
+            gu_half(1, layer, j)
+
+        @pl.when(low & ((r == 1) | (r == 2)))
         def _():
             pl.when(i == LOW + 1)(lambda: a0_load().wait())
-            loop(jnp.where(top, 0, r - 1), jnp.where(top, 2, r), lambda t: gu_half(t, layer, j))
+            gu_half(r - 1, layer, j)
 
         @pl.when((top | low) & (r == 3))
         def _():
@@ -537,20 +545,21 @@
             sums = at(half, HALF)
             acc[sums] = jnp.where(j == 0, 0.0, acc[sums]) + _dot(dgu[at(x, HALF)], wgu[x], 1, 1)
 
-            @pl.when(j == BLOCKS - 1)
+            @pl.when((j == BLOCKS - 1) | (u == BLOCKS))
             def _():
-                pl.when(half == 0)(lambda: h1_load().wait())
+                pl.when(u < BLOCKS)(lambda: h1_load().wait())
 
                 def one(t):
-                    there = pl.ds(pl.multiple_of(half * HALF + t * 256, 256), 256)
+                    there = at(t, 256)
                     wide, da = f(av[there]), acc[there]
                     scale = lax.rsqrt(jnp.mean(wide * wide, -1, keepdims=True) + 1e-6)
                     inner = jnp.mean(wide * da, -1, keepdims=True)
                     back = (scale * da - wide * (scale * scale * scale * inner)).astype(BF)
                     dv[there] = (f(dv[there]) + f(back)).astype(BF)
 
-                loop(0, HALF // 256, one)
-                pl.when(half == 1)(lambda: a0_load().start())
+                lo = jnp.where(u < BLOCKS, 0, jnp.where(u == BLOCKS, 2, 4))
+                loop(lo, lo + jnp.where(u > BLOCKS, 4, 2), one)
+                pl.when(u > BLOCKS)(lambda: a0_load().start())
 
         @pl.when(i == LOW - 2)
         def _():
@@ -569,8 +578,9 @@
         av[at(t, TT)] = _rms(dgu[at(t, TT), :D])
 
     loop(0, TILES, norm)
-    loop(0, STEPS - TILES + 1, functools.partial(forward, False))
-    loop(STEPS - TILES + 1, STEPS, functools.partial(forward, True))
+    loop(0, STEPS // 2 - 2, forward)
+    forward(STEPS // 2 - 2, (1,))
+    forward(STEPS // 2 - 1, (0, 1))
     down(STEPS - 1)
     close(TILES - 1)
     for s in range(STEPS - 3, STEPS):

time: 469 us -> 464 us (0.989)
  no operation moved by 1% of the time
where the time goes in v4:
time: 464 us
  Pallas kernels  463 us (100%)
    pallas_call x1, Pallas kernels, step_of(): pl.pallas_call(step_kernel, out_shape=outs, in_specs=hbm(len(args)), out_...  429 us
    pallas_call x1, Pallas kernels, copied(): pl.pallas_call(functools.partial(copy_kernel, n), out_shape=[jax.ShapeDty...  33.3 us

profile of v4, /device:TPU:0, one launch (start us, length us, event | category | flops | bytes accessed | tf_op | source)
XLA Modules:
  0.0 463.6 jit_solution(16092064274039464339)
XLA Ops:
  0.6 429.5 %shard_map.178 = (bf16[2,2,4,2,64,3200]{5,4,3,2,1,0:T(8,128)(2,1)}, bf16[2,2,4,2,64,3200]{5,4,3,2,1,0:T(8,128)(2,1)}, bf16[2,2,4,2,200,1024]{5,4,3,2,1,0:T(8,128...) custom-call(bf16[2048,1024]{1,0:T(8,128)(2,1)} %bitcast.14, ...), custom_call_target="tpu_custom_call" | custom-call | tf_op jit(solution)/shard_map/pallas_call | solution.py:630
  430.2 33.3 %shard_map.179 = (bf16[2,1024,3200]{2,1,0:T(8,128)(2,1)}, bf16[2,1024,3200]{2,1,0:T(8,128)(2,1)}, bf16[2,3200,1024]{2,1,0:T(8,128)(2,1)}, f32[2,64,3200]{2,1,0:T...) custom-call(bf16[2,1024,3200]{2,1,0:T(8,128)(2,1)} %bitcast.11, ...), custom_call_target="tpu_custom_call" | custom-call | tf_op jit(solution)/shard_map/pallas_call | solution.py:659
